TPU v7x, 128 devices: a whole 4x4x4 slice. The times are simulated.
128 devices in a mesh: data: 64 (over z, y, x), stage: 2 (over core).
Axes of the slice: x: 4, y: 4, z: 4, core: 2. Of those that a mesh axis runs over, the one named last changes fastest.
Arguments:
- act_in: bfloat16 [32, 64, 8, 512], P(None, 'data')
- cot_out: bfloat16 [32, 64, 8, 512], P(None, 'data')
- w_gate: bfloat16 [2, 2, 512, 2048], P(None, 'stage', 'data')
- w_in: bfloat16 [2, 2, 512, 2048], P(None, 'stage', 'data')
- w_out: bfloat16 [2, 2, 2048, 512], P(None, 'stage', 'data')
Outputs:
- output 1: bfloat16 [32, 64, 8, 512], P(None, 'data')
- output 2: float32 [2, 2, 512, 2048], P(None, 'stage', 'data')
- output 3: float32 [2, 2, 512, 2048], P(None, 'stage', 'data')
- output 4: float32 [2, 2, 2048, 512], P(None, 'stage', 'data')
All inputs are finite; a program needn't handle non-finite values.
Results may differ from a plain program's by a relative error of at most 0.0108.
Values are sent between devices in bfloat16 or wider.
A program may use at most 1 GiB of HBM per device.

v0:
```python
import jax
import jax.numpy as jnp
from jax import lax
from jax.sharding import PartitionSpec as P

NORM_EPS = 1e-6


def contract_rows(left, right):
    return lax.dot_general(left, right, (((0,), (0,)), ((), ())), preferred_element_type=jnp.float32)


def contract_cols(left, right):
    return lax.dot_general(left, right, (((1,), (1,)), ((), ())), preferred_element_type=jnp.float32)


def pick_at(stack, index):
    return lax.dynamic_index_in_dim(stack, index, keepdims=False)


def layer_forward(rows_in, gate_w, lin_w, proj_w):
    rows_f32 = rows_in.astype(jnp.float32)
    inv_rms = lax.rsqrt(jnp.mean(rows_f32 * rows_f32, axis=-1, keepdims=True) + NORM_EPS)
    normed = (rows_f32 * inv_rms).astype(jnp.bfloat16)
    gate_pre = jnp.dot(normed, gate_w, preferred_element_type=jnp.float32)
    lin_pre = jnp.dot(normed, lin_w, preferred_element_type=jnp.float32)
    gate_act = gate_pre * jax.nn.sigmoid(gate_pre)
    hidden = (gate_act * lin_pre).astype(jnp.bfloat16)
    proj_out = jnp.dot(hidden, proj_w, preferred_element_type=jnp.float32)
    return (rows_f32 + proj_out).astype(jnp.bfloat16)


def layer_backward(rows_in, grad_rows, gate_w, lin_w, proj_w):
    rows_f32 = rows_in.astype(jnp.float32)
    inv_rms = lax.rsqrt(jnp.mean(rows_f32 * rows_f32, axis=-1, keepdims=True) + NORM_EPS)
    scaled = rows_f32 * inv_rms
    normed = scaled.astype(jnp.bfloat16)
    gate_pre = jnp.dot(normed, gate_w, preferred_element_type=jnp.float32)
    lin_pre = jnp.dot(normed, lin_w, preferred_element_type=jnp.float32)
    gate_sig = jax.nn.sigmoid(gate_pre)
    gate_act = gate_pre * gate_sig
    hidden = (gate_act * lin_pre).astype(jnp.bfloat16)
    grad_proj = contract_rows(hidden, grad_rows)
    grad_hidden = contract_cols(grad_rows, proj_w)
    d_gate = (grad_hidden * lin_pre * gate_sig * (1.0 + gate_pre * (1.0 - gate_sig))).astype(jnp.bfloat16)
    d_lin = (grad_hidden * gate_act).astype(jnp.bfloat16)
    grad_gate = contract_rows(normed, d_gate)
    grad_lin = contract_rows(normed, d_lin)
    grad_norm = contract_cols(d_gate, gate_w) + contract_cols(d_lin, lin_w)
    grad_in = grad_rows.astype(jnp.float32) + inv_rms * (grad_norm - scaled * jnp.mean(grad_norm * scaled, axis=-1, keepdims=True))
    return grad_in.astype(jnp.bfloat16), grad_gate, grad_lin, grad_proj


def solution(mesh):
    stage_n = mesh.shape["stage"]
    fwd_perm = [(src, (src + 1) % stage_n) for src in range(stage_n)]
    bwd_perm = [(src, (src - 1) % stage_n) for src in range(stage_n)]
    act_spec = P(None, "data", None, None)
    w_spec = P(None, "stage", "data", None)

    def body(act_in, cot_out, w_gate, w_in, w_out):
        n_micro, rows_dev, seq_len, dmodel = act_in.shape
        ffn_dim = w_gate.shape[3]
        tok_rows = rows_dev * seq_len
        act_micro = act_in.reshape(n_micro, tok_rows, dmodel)
        cot_micro = cot_out.reshape(n_micro, tok_rows, dmodel)
        gate_full = lax.all_gather(w_gate[:, 0], "data", axis=1, tiled=True)
        lin_full = lax.all_gather(w_in[:, 0], "data", axis=1, tiled=True)
        proj_full = lax.all_gather(w_out[:, 0], "data", axis=1, tiled=True)
        stage_idx = lax.axis_index("stage")
        n_steps = 2 * n_micro
        round_len = 2 * stage_n
        tick_ids = jnp.arange(n_steps + stage_n - 1)

        def fwd_tick(recv_rows, tick_idx):
            step_idx = jnp.clip(tick_idx - stage_idx, 0, n_steps - 1)
            virt_idx = (step_idx % round_len) // stage_n
            micro_idx = (step_idx // round_len) * stage_n + step_idx % stage_n
            layer_in = jnp.where((virt_idx == 0) & (stage_idx == 0), pick_at(act_micro, micro_idx), recv_rows)
            layer_out = layer_forward(layer_in, pick_at(gate_full, virt_idx), pick_at(lin_full, virt_idx), pick_at(proj_full, virt_idx))
            return lax.ppermute(layer_out, "stage", fwd_perm), layer_in

        zero_rows = jnp.zeros((tok_rows, dmodel), jnp.bfloat16)
        last_fwd, seen_in = lax.scan(fwd_tick, zero_rows, tick_ids)
        saved_in = lax.dynamic_slice_in_dim(seen_in, stage_idx, n_steps, axis=0)

        def bwd_tick(carry_in, tick_idx):
            recv_rows, acc_gate, acc_lin, acc_proj = carry_in
            raw_step = tick_idx - (stage_n - 1 - stage_idx)
            is_valid = (raw_step >= 0) & (raw_step < n_steps)
            step_idx = jnp.clip(raw_step, 0, n_steps - 1)
            group_idx = step_idx // round_len
            within = step_idx % round_len
            virt_idx = 1 - within // stage_n
            slot_idx = within % stage_n
            micro_idx = group_idx * stage_n + slot_idx
            fwd_pos = group_idx * round_len + virt_idx * stage_n + slot_idx
            grad_out = jnp.where((virt_idx == 1) & (stage_idx == stage_n - 1), pick_at(cot_micro, micro_idx), recv_rows)
            grad_out = jnp.where(is_valid, grad_out, jnp.zeros_like(grad_out))
            grad_in, grad_g, grad_l, grad_p = layer_backward(pick_at(saved_in, fwd_pos), grad_out, pick_at(gate_full, virt_idx), pick_at(lin_full, virt_idx), pick_at(proj_full, virt_idx))
            acc_gate = lax.dynamic_update_index_in_dim(acc_gate, pick_at(acc_gate, virt_idx) + grad_g, virt_idx, 0)
            acc_lin = lax.dynamic_update_index_in_dim(acc_lin, pick_at(acc_lin, virt_idx) + grad_l, virt_idx, 0)
            acc_proj = lax.dynamic_update_index_in_dim(acc_proj, pick_at(acc_proj, virt_idx) + grad_p, virt_idx, 0)
            return (lax.ppermute(grad_in, "stage", bwd_perm), acc_gate, acc_lin, acc_proj), grad_in

        zero_up = jnp.zeros((2, dmodel, ffn_dim), jnp.float32)
        zero_down = jnp.zeros((2, ffn_dim, dmodel), jnp.float32)
        carry_out, seen_grad = lax.scan(bwd_tick, (zero_rows, zero_up, zero_up, zero_down), tick_ids)
        first_grad = seen_grad[stage_n - 1:stage_n - 1 + n_steps].reshape(n_micro // stage_n, 2, stage_n, tok_rows, dmodel)[:, 1]
        first_grad = jnp.where(stage_idx == 0, first_grad, jnp.zeros_like(first_grad))
        grad_act = lax.psum(first_grad, "stage").reshape(n_micro, rows_dev, seq_len, dmodel)
        grad_gate = lax.psum_scatter(carry_out[1], "data", scatter_dimension=1, tiled=True)[:, None]
        grad_lin = lax.psum_scatter(carry_out[2], "data", scatter_dimension=1, tiled=True)[:, None]
        grad_proj = lax.psum_scatter(carry_out[3], "data", scatter_dimension=1, tiled=True)[:, None]
        return grad_act, grad_gate, grad_lin, grad_proj

    return jax.shard_map(body, mesh=mesh, in_specs=(act_spec, act_spec, w_spec, w_spec, w_spec), out_specs=(act_spec, w_spec, w_spec, w_spec), check_vma=False)
```

profile of v0, /device:TPU:0, one launch (start us, length us, event | category | flops | bytes accessed | tf_op | source)
XLA Modules:
  0.0 3837.1 jit_solution(9777090571945313797)
XLA Ops:
  9.4 72.7 %all-gather.7.cloned.1.call-done = bf16[2,1,512,2048]{3,2,0,1:T(8,128)(2,1)} async-done(((bf16[2,1,8,2048]{3,2,0,1:T(8,128)(2,1)}), bf16[2,1,512,2048]{3,2,0,1:T(8,128)(2,1)}) %all-gather.7.cloned.1.call-update) | async-done | bytes 4194320 | tf_op jit(solution)/shard_map/all_gather | solution.py:67
  82.1 69.0 %all-gather.9.cloned.1.call-done = bf16[2,1,512,2048]{3,2,0,1:T(8,128)(2,1)} async-done(((bf16[2,1,8,2048]{3,2,0,1:T(8,128)(2,1)}), bf16[2,1,512,2048]{3,2,0,1:T(8,128)(2,1)}) %all-gather.9.cloned.1.call-update) | async-done | bytes 4194320 | tf_op jit(solution)/shard_map/all_gather | solution.py:68
  151.1 69.0 %all-gather.11.cloned.1.call-done = bf16[2,1,2048,512]{3,2,0,1:T(8,128)(2,1)} async-done(((bf16[2,1,32,512]{3,2,0,1:T(8,128)(2,1)}), bf16[2,1,2048,512]{3,2,0,1:T(8,128)(2,1)}) %all-gather.11.cloned.1.call-update) | async-done | bytes 4194320 | tf_op jit(solution)/shard_map/all_gather | solution.py:69
  220.1 525.6 %while.36 = (s32[]{:T(128)}, bf16[8,512]{1,0:T(8,128)(2,1)S(1)}, bf16[65,8,512]{2,1,0:T(8,128)(2,1)S(1)}, s32[65]{0:T(128)S(1)}, s32[]{:T(128)}, /*index=5*/pred...) while((s32[]{:T(128)}, bf16[8,512]{1,0:T(8,128)(2,1)S(1)}, ...), condition=%wide.region_2.3_spmd, body=%wide.region_0.2_spmd.sunk | while | flops 50483256 | bytes 6531381 | solution.py:84
  745.8 4.3 broadcast_in_dim.59.clone
  750.1 4.3 broadcast_in_dim.60
  754.4 4.3 broadcast_in_dim.59
  758.7 1937.2 %while.37 = (s32[]{:T(128)}, bf16[8,512]{1,0:T(8,128)(2,1)S(1)}, f32[2,512,2048]{2,1,0:T(8,128)}, f32[2,512,2048]{2,1,0:T(8,128)}, f32[2,2048,512]{2,1,0:T(8,128...) while((s32[]{:T(128)}, bf16[8,512]{1,0:T(8,128)(2,1)S(1)}, ...), condition=%wide.region_6.7_spmd, body=%wide.region_3.6_spmd.sunk | while | flops 137797696 | bytes 204239600 | solution.py:108
  804.8 3.5 copy-done.3
  864.4 3.5 copy-done.3
  953.8 3.5 copy-done.3
  983.6 3.5 copy-done.3
  1073.1 3.5 copy-done.3
  1102.8 3.5 copy-done.3
  1192.3 3.5 copy-done.3
  1222.1 3.5 copy-done.3
  1311.5 3.5 copy-done.3
  1341.3 3.5 copy-done.3
  1400.9 3.5 copy-done.3
  1430.7 3.5 copy-done.3
  1460.5 3.5 copy-done.3
  1520.1 3.5 copy-done.3
  1549.9 3.5 copy-done.3
  1579.7 3.5 copy-done.3
  1639.4 3.5 copy-done.3
  1669.1 3.5 copy-done.3
  1698.9 3.5 copy-done.3
  1788.4 3.5 copy-done.3
  1818.1 3.5 copy-done.3
  1907.6 3.5 copy-done.3
  1937.4 3.5 copy-done.3
  2026.8 3.5 copy-done.3
  2056.6 3.5 copy-done.3
  2146.0 3.5 copy-done.3
  2175.8 3.5 copy-done.3
  2265.2 3.5 copy-done.3
  2295.0 3.5 copy-done.3
  2384.4 3.5 copy-done.3
  2414.2 3.5 copy-done.3
  2503.7 3.5 copy-done.3
  2533.4 3.5 copy-done.3
  2593.1 3.5 copy-done.3
  2622.9 3.5 copy-done.3
  2652.7 3.5 copy-done.3
  2698.6 19.2 all-reduce.2.cloned.1.call-done
  2717.8 374.6 %reduce-scatter.8.cloned.1.call-done = f32[2,32,512]{2,1,0:T(8,128)} async-done(((f32[2,2048,512]{2,1,0:T(8,128)}), f32[2,32,512]{2,1,0:T(8,128)}) %reduce-scatter.8.cloned.1.call-update) | async-done | bytes 131088 | tf_op jit(solution)/shard_map/reduce_scatter | solution.py:114
  3092.4 368.2 %reduce-scatter.4.cloned.1.call-done = f32[2,8,2048]{2,1,0:T(8,128)} async-done(((f32[2,512,2048]{2,1,0:T(8,128)}), f32[2,8,2048]{2,1,0:T(8,128)}) %reduce-scatter.4.cloned.1.call-update) | async-done | bytes 131088 | tf_op jit(solution)/shard_map/reduce_scatter | solution.py:112
  3460.6 368.0 %reduce-scatter.6.cloned.1.call-done = f32[2,8,2048]{2,1,0:T(8,128)} async-done(((f32[2,512,2048]{2,1,0:T(8,128)}), f32[2,8,2048]{2,1,0:T(8,128)}) %reduce-scatter.6.cloned.1.call-update) | async-done | bytes 131088 | tf_op jit(solution)/shard_map/reduce_scatter | solution.py:113
  (2523 shorter events, 2254.1 us)
Async XLA Ops:
  7.2 74.9 %all-gather.7.cloned.1.call-start = ((), (), s32[]{:S(2)}) async-start(), calls=%async_computation.7 | async-start | bytes 4259840 | tf_op jit(solution)/shard_map/all_gather | solution.py:67
  7.9 143.2 %all-gather.9.cloned.1.call-start = ((), (), s32[]{:S(2)}) async-start(), calls=%async_computation.8 | async-start | bytes 4259840 | tf_op jit(solution)/shard_map/all_gather | solution.py:68
  8.6 211.4 %all-gather.11.cloned.1.call-start = ((), (), s32[]{:S(2)}) async-start(), calls=%async_computation.9 | async-start | bytes 4259840 | tf_op jit(solution)/shard_map/all_gather | solution.py:69
  9.4 2708.4 %all-reduce.2.cloned.1.call-start = ((), (), s32[]{:S(2)}) async-start(), calls=%async_computation.3 | async-start | bytes 524288 | tf_op jit(solution)/shard_map/psum | solution.py:111
  800.3 17.9 collective-permute-start.1
  859.9 18.0 collective-permute-start.1
  889.7 18.0 collective-permute-start.1
  979.1 18.0 collective-permute-start.1
  1008.9 18.0 collective-permute-start.1
  1038.7 17.9 collective-permute-start.1
  1098.3 18.0 collective-permute-start.1
  1128.1 18.0 collective-permute-start.1
  1157.9 17.9 collective-permute-start.1
  1217.5 18.0 collective-permute-start.1
  1247.3 18.0 collective-permute-start.1
  1277.1 17.9 collective-permute-start.1
  1336.7 18.0 collective-permute-start.1
  1366.5 18.0 collective-permute-start.1
  1396.4 17.9 collective-permute-start.1
  1455.9 18.0 collective-permute-start.1
  1485.8 18.0 collective-permute-start.1
  1515.6 17.9 collective-permute-start.1
  1575.2 18.0 collective-permute-start.1
  1605.0 18.0 collective-permute-start.1
  1634.8 17.9 collective-permute-start.1
  1694.4 18.0 collective-permute-start.1
  1724.2 18.0 collective-permute-start.1
  1754.0 17.9 collective-permute-start.1
  1813.6 18.0 collective-permute-start.1
  1843.4 18.0 collective-permute-start.1
  1932.8 18.0 collective-permute-start.1
  1962.6 18.0 collective-permute-start.1
  1992.4 17.9 collective-permute-start.1
  2052.0 18.0 collective-permute-start.1
  2081.8 18.0 collective-permute-start.1
  2171.2 18.0 collective-permute-start.1
  2201.1 18.0 collective-permute-start.1
  2290.5 18.0 collective-permute-start.1
  2320.3 18.0 collective-permute-start.1
  2409.7 18.0 collective-permute-start.1
  2439.5 18.0 collective-permute-start.1
  2528.9 18.0 collective-permute-start.1
  2558.7 18.0 collective-permute-start.1
  2648.1 18.0 collective-permute-start.1
  2677.9 18.0 collective-permute-start.1
  2696.7 395.7 %reduce-scatter.8.cloned.1.call-start = ((), (), s32[]{:S(2)}) async-start(), calls=%async_computation.6 | async-start | bytes 8519680 | tf_op jit(solution)/shard_map/reduce_scatter | solution.py:114
  2697.3 763.4 %reduce-scatter.4.cloned.1.call-start = ((), (), s32[]{:S(2)}) async-start(), calls=%async_computation.4 | async-start | bytes 8519680 | tf_op jit(solution)/shard_map/reduce_scatter | solution.py:112
  2697.8 1130.8 %reduce-scatter.6.cloned.1.call-start = ((), (), s32[]{:S(2)}) async-start(), calls=%async_computation.5 | async-start | bytes 8519680 | tf_op jit(solution)/shard_map/reduce_scatter | solution.py:113
  (479 other events, 2397.1 us)
Sparse Core Ops, SparseCore 0:
  10.9 71.1 all-gather.6
  85.0 66.0 all-gather.8
  154.0 66.0 all-gather.10
  2696.8 20.9 all-reduce.1
  2720.6 371.7 reduce-scatter.7
  3095.2 365.3 reduce-scatter.3
  3463.6 364.9 reduce-scatter.5
where the time goes:
time: 3850 us; the launch traced here: 3840 us
  waiting for transfers between devices  1410 us (37%)
  matrix products  1220 us (32%)
  local copies, waits for them, and re-layouts  955 us (25%)
  other arithmetic  125 us (3%)
  loops' own time  89.2 us (2%)
    while x780, local copies, waits for them, and re-layouts  468 us
    dynamic_slice x130, local copies, waits for them, and re-layouts, pick_at(): return lax.dynamic_index_in_dim(stack, index, keepdims=False)  398 us
    reduce_scatter x1, waiting for transfers between devices, body(): lax.psum_scatter(carry_out[3], 'data', scatter_dimension=1, tiled=True)  375 us
    reduce_scatter x1, waiting for transfers between devices, body(): lax.psum_scatter(carry_out[1], 'data', scatter_dimension=1, tiled=True)  368 us
    reduce_scatter x1, waiting for transfers between devices, body(): lax.psum_scatter(carry_out[2], 'data', scatter_dimension=1, tiled=True)  368 us
    dot_general x195, matrix products, contract_cols(): lax.dot_general(left, right, (((1,), (1,)), ((), ())), preferred_element_...  354 us
    dot_general x195, matrix products, contract_rows(): lax.dot_general(left, right, (((0,), (0,)), ((), ())), preferred_element_...  283 us
    dot_general x65, matrix products, layer_forward(): proj_out = jnp.dot(hidden, proj_w, preferred_element_type=jnp.float32)  189 us
  transfers between devices with their start and end apart: 137, of which 72 were waited for; matrix products, arithmetic and copies ran while one was open for 18% of the time, Pallas kernels for 0%

commit v1 on v0

v1 whole, which is shorter than its diff:
```python
import functools

import jax
import jax.numpy as jnp
from jax import lax
from jax.experimental import pallas as pl
from jax.experimental.pallas import tpu as pltpu
from jax.sharding import PartitionSpec as P

NORM_EPS = 1e-6
BF = jnp.bfloat16
F32 = jnp.float32
MESH = pl.DeviceIdType.MESH
X, Y, Z = 0, 1, 2
BLOCKS = COLOURS = HALVES = (0, 1)
NB, NA, NL = len(BLOCKS), 4, 64
RING = (1, 3, 2)
OPP = RING[-1]
PLUS, MINUS = RING[:-1]
QUARTERS = range(NA)
AXES = ((X, Y, Z), (Y, Z, X), (Z, X, Y))


def mm(left, right):
    return jnp.dot(left, right, preferred_element_type=F32)


def mm_nt(left, right):
    return lax.dot_general(left, right, (((1,), (1,)), ((), ())), preferred_element_type=F32)


def mm_tn(left, right):
    return lax.dot_general(left, right, (((0,), (0,)), ((), ())), preferred_element_type=F32)


def inv_rms(h):
    return lax.rsqrt(jnp.mean(h * h, axis=-1, keepdims=True) + NORM_EPS)


def kernel(act, cot, wg_in, wi_in, wo_in, gact, gg, gi, go,
           wg, wi, wo, hb, eb, xo, ga, ng, f1, f2, f1s, f2s, us, ub, da, db, das, dbs, qs, gs, is_, os_,
           gin, gout, fin, r3,
           lsem, ag_s, ag_r, lg_r, mc_s, mc_r, rl_s, ga_s, ga_r, rs_s, rs_r, r3_s, r3_r, turn, *rg):
    dm, fd = wo.shape[-1], wg.shape[-1]
    dr, fr = dm // NL, fd // NL
    fs = fd // NA
    pf = fs // NA
    rows = act.shape[0]
    wts = (wg, wi, wo)

    p = lax.axis_index("stage")
    d = lax.axis_index("data")
    zc, yc, xc = lax.div(d, 16), lax.rem(lax.div(d, 4), 4), lax.rem(d, 4)
    coord = (xc, yc, zc)
    stride = (1, 4, 16)
    ja = yc + p * (zc - yc)
    jb = zc + p * (yc - zc)
    sa, sb = 4 + 12 * p, 16 - 12 * p

    def rot(c, delta):
        return lax.rem(c + (delta % 4), 4)

    def peer(ax, delta):
        return d + (rot(coord[ax], delta) - coord[ax]) * stride[ax]

    def peer_a(delta):
        return d + (rot(ja, delta) - ja) * sa

    def peer_b(delta):
        return d + (rot(jb, delta) - jb) * sb

    def remote(src, dst, ssem, rsem, dev, core):
        return pltpu.make_async_remote_copy(src_ref=src, dst_ref=dst, send_sem=ssem, recv_sem=rsem,
                                            device_id=(dev, core), device_id_type=MESH)

    def send(src, dst, ssem, rsem, dev, core):
        remote(src, dst, ssem, rsem, dev, core).start()

    def wait_recv(ref, sem):
        remote(ref, ref, sem, sem, d, p).wait_recv()

    def wait_send(ref, sem):
        remote(ref, ref, sem, sem, d, p).wait_send()

    for v in BLOCKS:
        for k, shard in enumerate((wg_in, wi_in, wo_in)):
            pltpu.make_async_copy(shard.at[v], wts[k].at[v, zc, yc, xc], lsem.at[v, k]).start()

    @pl.when(p == 0)
    def _():
        pltpu.make_async_copy(act, hb.at[0, ja], lsem.at[0, 3]).start()

    @pl.when(p == 1)
    def _():
        pltpu.make_async_copy(cot, eb.at[1, ja], lsem.at[0, 3]).start()

    barrier = pltpu.get_barrier_semaphore()
    senders = [(peer(ax, delta), p) for ax in (X, Y, Z) for delta in RING]
    senders += [(d, 1 - p), (peer_a(1), 1 - p), (peer_a(-1), 1 - p)]
    for dev, core in senders:
        pl.semaphore_signal(barrier, inc=1, device_id=(dev, core), device_id_type=MESH)
    for v in BLOCKS:
        for k, shard in enumerate((wg_in, wi_in, wo_in)):
            pltpu.make_async_copy(shard.at[v], wts[k].at[v, zc, yc, xc], lsem.at[v, k]).wait()

    @pl.when(p == 0)
    def _():
        pltpu.make_async_copy(act, hb.at[0, ja], lsem.at[0, 3]).wait()

    @pl.when(p == 1)
    def _():
        pltpu.make_async_copy(cot, eb.at[1, ja], lsem.at[0, 3]).wait()

    pl.semaphore_wait(barrier, len(senders))

    FIRST, REST = ((0, PLUS, 0), (1, MINUS, 2)), ((1, PLUS, 1), (0, MINUS, 3))
    LARGE = 2

    def chunk(v, k, ph, q, half):
        if ph == 0:
            width = wts[k].shape[-1] // 2
            ix = tuple(q if ax == AXES[k][0] else coord[ax] for ax in (Z, Y, X)) + (slice(None), pl.ds(half * width, width))
        else:
            hs = pl.ds(2 * half, 2)
            ix = ((zc, q, hs), (q, hs, xc), (hs, yc, q))[k]
        return wts[k].at[(v,) + ix]

    def small_copy(v, k, ph, q, half, delta, slot):
        ref = chunk(v, k, ph, q, half)
        send(ref, ref, ag_s.at[v, k, ph], ag_r.at[v, k, ph, slot], peer(AXES[k][ph], delta), p)

    def small_wait(v, k, ph, back, half, slot):
        wait_recv(chunk(v, k, ph, rot(coord[AXES[k][ph]], back), half), ag_r.at[v, k, ph, slot])

    def small_send(v, ph):
        for half, delta, slot in FIRST + REST:
            for k in (X, Y, Z):
                small_copy(v, k, ph, coord[AXES[k][ph]], half, delta, slot)

    def small_relay(v, ph):
        for half, delta, slot in FIRST:
            for k in (X, Y, Z):
                small_wait(v, k, ph, -delta, half, slot)
                small_copy(v, k, ph, rot(coord[AXES[k][ph]], -delta), half, delta, 4 + half)

    def small_rest(v, ph):
        for half, delta, slot in REST:
            for k in (X, Y, Z):
                small_wait(v, k, ph, -delta, half, slot)

    def small_last(v, ph):
        for half in HALVES:
            for k in (X, Y, Z):
                small_wait(v, k, ph, OPP, half, 4 + half)

    UP, DOWN = (0, PLUS), (MINUS, OPP)
    RELAYS = ((UP[0], PLUS), (DOWN[0], MINUS), (UP[1], PLUS), (DOWN[1], MINUS))

    def row(v, k, q, r):
        m = rot(coord[AXES[k][1]], r)
        ix = ((q, m), (m, slice(None), q), (slice(None), q, m))[k]
        return wts[k].at[(v,) + ix]

    def large_slot(r, delta):
        return r if delta == PLUS else NA + r

    def large_send(v, up, down):
        for pair in zip(up, down):
            for r, delta in zip(pair, (PLUS, MINUS)):
                for k in (X, Y, Z):
                    ax = AXES[k][LARGE]
                    ref = row(v, k, coord[ax], r)
                    send(ref, ref, ag_s.at[v, k, LARGE], lg_r.at[v, k, large_slot(r, delta)], peer(ax, delta), p)

    def large_relay(v):
        for r, delta in RELAYS:
            for k in (X, Y, Z):
                ax = AXES[k][LARGE]
                ref = row(v, k, rot(coord[ax], -delta), r)
                wait_recv(ref, lg_r.at[v, k, large_slot(r, delta)])
                send(ref, ref, ag_s.at[v, k, LARGE], lg_r.at[v, k, 2 * NA + r], peer(ax, delta), p)

    def large_finish(v):
        for pieces, delta in ((DOWN, PLUS), (UP, MINUS)):
            for r in pieces:
                for k in (X, Y, Z):
                    wait_recv(row(v, k, rot(coord[AXES[k][LARGE]], -delta), r), lg_r.at[v, k, large_slot(r, delta)])
        for r in QUARTERS:
            for k in (X, Y, Z):
                wait_recv(row(v, k, rot(coord[AXES[k][LARGE]], OPP), r), lg_r.at[v, k, 2 * NA + r])

    half_rows = rows // 2

    def spread_near(src, buf, which, vd, ssem):
        send(src, buf.at[vd, jb], ssem, mc_r.at[which, vd, 0], d, 1 - p)

    def spread_far(src, buf, which, vd, ssem):
        send(src, buf.at[vd, jb], ssem, mc_r.at[which, vd, 1], peer_b(1), 1 - p)
        send(src, buf.at[vd, jb], ssem, mc_r.at[which, vd, 2], peer_b(-1), 1 - p)

    def spread_same(buf, which, v, ssem):
        own = buf.at[v, ja]
        send(own, own, ssem, mc_r.at[which, v, 1], peer_a(1), p)
        send(own, own, ssem, mc_r.at[which, v, 2], peer_a(-1), p)

    def spread_relay(buf, which, v):
        for half, delta in ((0, 1), (1, 3)):
            slot = rot(ja, -delta)
            wait_recv(buf.at[v, slot], mc_r.at[which, v, 1 + half])
            ref = buf.at[v, slot, pl.ds(half * half_rows, half_rows)]
            send(ref, ref, rl_s.at[which, v], mc_r.at[which, v, 3 + half], peer_a(delta), p)

    def spread_finish(buf, which, v):
        for half in HALVES:
            wait_recv(buf.at[v, rot(ja, 2), pl.ds(half * half_rows, half_rows)], mc_r.at[which, v, 3 + half])

    def spread_own(buf, which, v):
        wait_recv(buf.at[v, ja], mc_r.at[which, v, 0])

    def gates(n, wgt, wlin):
        a, b = mm(n, wgt), mm(n, wlin)
        s = jax.nn.sigmoid(a)
        act_a = a * s
        return (act_a * b).astype(BF), b * s * (1.0 + a * (1.0 - s)), act_a

    def block_gates(v):
        h = hb[v, ja].astype(F32)
        n = (h * inv_rms(h)).astype(BF)

        def tile(i, carry):
            wide = fs // 2
            cols = pl.ds(pl.multiple_of(i * wide, wide), wide)
            u, t1, t2 = gates(n, wg[v, :, :, :, :, cols].reshape(dm, wide), wi[v, :, :, :, :, cols].reshape(dm, wide))
            ub[:, cols] = u
            f1[v, :, cols] = t1
            f2[v, :, cols] = t2
            return carry

        lax.fori_loop(0, 2 * NA, tile, 0, unroll=True)

    def block_out(v, dst):
        half_dm = dm // 2
        for i in HALVES:
            cols = pl.ds(i * half_dm, half_dm)
            out = mm(ub[...], wo[v, :, :, :, :, cols].reshape(fd, half_dm))
            dst[:, cols] = (hb[v, ja, :, cols].astype(F32) + out).astype(BF)

    def block_backward(v, dst):
        e = eb[v, ja]

        def tile(i, carry):
            cols = pl.ds(pl.multiple_of(i * fs, fs), fs)
            t = mm_nt(e, wo[v, i].reshape(fs, dm))
            da[:, cols] = (t * f1[v, :, cols]).astype(BF)
            db[:, cols] = (t * f2[v, :, cols]).astype(BF)
            return carry

        lax.fori_loop(0, NA, tile, 0, unroll=True)
        half_dm = dm // 2
        for i in HALVES:
            q = mm_nt(da[...], wg[v, pl.ds(2 * i, 2)].reshape(half_dm, fd))
            q += mm_nt(db[...], wi[v, pl.ds(2 * i, 2)].reshape(half_dm, fd))
            qs[:, pl.ds(i * half_dm, half_dm)] = q
        h = hb[v, ja].astype(F32)
        r = inv_rms(h)
        hr = h * r
        q = qs[...]
        dst[...] = (e.astype(F32) + r * (q - hr * jnp.mean(q * hr, axis=-1, keepdims=True))).astype(BF)

    def piece(j, i):
        z = i + p * (j - i)
        y = j + p * (i - j)
        return z, y

    def grad_first(v):
        for i in QUARTERS:
            z, y = piece(ja, i)
            cols = pl.ds(pl.multiple_of((z * NA + y) * pf, pf), pf)
            gs[:, pl.ds(i * pf, pf)] = wg[v, :, :, :, :, cols].reshape(dm, pf)
            is_[:, pl.ds(i * pf, pf)] = wi[v, :, :, :, :, cols].reshape(dm, pf)

        def tile(s, carry):
            h = hb[v, s].astype(F32)
            n = (h * inv_rms(h)).astype(BF)
            ng[v, s] = n
            u, t1, t2 = gates(n, gs[...], is_[...])
            us[v, s] = u
            f1s[v, s] = t1
            f2s[v, s] = t2
            return carry

        lax.fori_loop(0, NA, tile, 0, unroll=True)

    def grad_hidden(v):
        for i in QUARTERS:
            z, y = piece(ja, i)
            os_[pl.ds(i * pf, pf), :] = wo[v, z, y].reshape(pf, dm)

        def tile(s, carry):
            t = mm_nt(eb[v, s], os_[...])
            das[s] = (t * f1s[v, s]).astype(BF)
            dbs[s] = (t * f2s[v, s]).astype(BF)
            return carry

        lax.fori_loop(0, NA, tile, 0, unroll=True)

    def grad_out(v):
        def tile(i, carry):
            cols = pl.ds(pl.multiple_of(i * 2 * pf, 2 * pf), 2 * pf)
            g = mm_tn(us[v, :, :, cols].reshape(NA * rows, 2 * pf), eb[v].reshape(NA * rows, dm))
            gout[v, pl.ds(2 * i, 2)] = g.reshape(2, 4, fr, dm)
            return carry

        lax.fori_loop(0, 2, tile, 0, unroll=True)

    def grad_in(v):
        for which, dref in enumerate((das, dbs)):

            def tile(i, carry, which=which, dref=dref):
                cols = pl.ds(pl.multiple_of(i * (dm // NA), dm // NA), dm // NA)
                g = mm_tn(ng[v, :, :, cols].reshape(NA * rows, dm // NA), dref[...].reshape(NA * rows, fs)).reshape(4, 4, dr, fs)

                for y in QUARTERS:
                    gin[v, which, y + p * (i - y), i + p * (y - i)] = g[y]
                return carry

            lax.fori_loop(0, NA, tile, 0, unroll=True)

    IN, OUT = 0, 1

    def split(width):
        return pl.ds(0, width - pf), pl.ds(width - pf, pf)

    def view(which, st, v, colour, t, half):
        along_b = colour == st
        if which == IN:
            cols = split(fs)[colour]
            b, x = (t, slice(None) if st == 0 else xc) if along_b else (slice(None) if st == 0 else jb, t)
            return gin.at[v, half, :, b, x, :, cols]
        cols = split(dm)[colour]
        if st == 0:
            hs = pl.ds(2 * half, 2)
            return gout.at[v, t, hs, :, cols] if along_b else gout.at[v, hs, t, :, cols]
        hs = pl.ds(half * (fr // 2), fr // 2)
        return gout.at[v, t, xc, hs, cols] if along_b else gout.at[v, jb, t, hs, cols]

    RECV = (((rg[0], rg[1]), (rg[2], rg[3])), ((rg[4], rg[5]), (rg[6], rg[7])))
    MERGED, DIRECT = ((0, OPP, PLUS, 0), (1, OPP, MINUS, 1)), ((1, PLUS, PLUS, 2), (0, MINUS, MINUS, 3))
    RELAYED = ((0, PLUS, PLUS, 4), (1, MINUS, MINUS, 5))

    def axis_of(colour, st):
        return (jb, peer_b) if colour == st else (xc, functools.partial(peer, X))

    def scatter_send(v, which, st, copies):
        for colour in COLOURS:
            q, to = axis_of(colour, st)
            for half, c, delta, slot in copies:
                send(view(which, st, v, colour, rot(q, c), half), RECV[st][which][colour].at[v, slot],
                     rs_s.at[st, v, colour, which], rs_r.at[st, v, colour, which, slot], to(delta), p)

    def scatter_relay(v, which, st):
        for colour in COLOURS:
            q, _ = axis_of(colour, st)
            recv = RECV[st][which][colour]
            for half, c, _, slot in RELAYED:
                wait_recv(recv.at[v, slot - 4], rs_r.at[st, v, colour, which, slot - 4])
                ref = view(which, st, v, colour, rot(q, c), half)
                ref[...] = ref[...] + recv[v, slot - 4]
        scatter_send(v, which, st, RELAYED)

    def scatter_sum(v, which, st):
        for colour in COLOURS:
            q, _ = axis_of(colour, st)
            recv = RECV[st][which][colour]
            for half in HALVES:
                direct, merged = 3 - half, 4 + half
                for slot in (direct, merged):
                    wait_recv(recv.at[v, slot], rs_r.at[st, v, colour, which, slot])
                ref = view(which, st, v, colour, q, half)
                ref[...] = ref[...] + recv[v, direct] + recv[v, merged]

    def scatter_turn(v, which):
        scatter_sum(v, which, 0)
        scatter_send(v, which, 1, MERGED + DIRECT)

    def scatter_last(v):
        scatter_sum(v, OUT, 1)
        go[v] = gout[v, jb, xc]
        scatter_sum(v, IN, 1)
        for which in HALVES:
            fin[v, :, which] = gin[v, which, :, jb, xc]
        for delta in RING:
            send(fin.at[v, rot(ja, delta)], r3.at[v, delta - 1], r3_s.at[v], r3_r.at[v, delta - 1], peer_a(delta), p)

    def scatter_finish(v):
        def put(j, vals):
            for i in QUARTERS:
                z, y = piece(j, i)
                cols = pl.ds(pl.multiple_of((z * NA + y) * pf, pf), pf)
                gg[v, :, cols] = vals(0)[:, i * pf:(i + 1) * pf]
                gi[v, :, cols] = vals(1)[:, i * pf:(i + 1) * pf]

        put(ja, lambda w: fin[v, ja, w])
        for delta in RING:
            wait_recv(r3.at[v, delta - 1], r3_r.at[v, delta - 1])
            put(rot(ja, -delta), lambda w, delta=delta: r3[v, delta - 1, w])

    def step(fn, *args):
        with jax.named_scope(fn.__name__):
            fn(*args)

    def on(core):
        return pl.when(p == core)

    def take_turn():
        pl.semaphore_wait(turn, 1)

    def give_turn():
        pl.semaphore_signal(turn, inc=1, device_id=(d, 1 - p), device_id_type=MESH)

    h_mid, h_late, e_first, e_last = ((xo.at[i], mc_s.at[1 + i]) for i in QUARTERS)

    def pass_on(part, item, buf, which, vd):
        step(part, item[0], buf, which, vd, item[1])

    ALL = UP + (MINUS, OPP), DOWN + (0, PLUS)
    for v in BLOCKS:
        step(small_send, v, 0)
    for v in BLOCKS:
        step(small_relay, v, 0)
    step(small_rest, 0, 0)
    step(small_last, 0, 0)
    step(small_send, 0, 1)
    step(large_send, 0, (0,), (0,))
    step(small_rest, 1, 0)
    step(small_last, 1, 0)
    step(small_send, 1, 1)
    step(small_relay, 0, 1)
    step(small_relay, 1, 1)
    step(small_rest, 0, 1)
    step(large_send, 0, (PLUS, MINUS), (MINUS, PLUS))
    step(small_last, 0, 1)
    step(large_send, 0, (OPP,), (OPP,))
    step(small_rest, 1, 1)
    step(small_last, 1, 1)
    step(large_relay, 0)

    @on(0)
    def _():
        step(large_send, 1, *ALL)

    step(large_finish, 0)

    @on(1)
    def _():
        step(spread_own, hb, 0, 0)

    step(block_gates, 0)
    step(block_out, 0, h_mid[0])
    pass_on(spread_near, h_mid, hb, 0, p)

    @on(1)
    def _():
        step(take_turn)
        step(large_send, 1, *ALL)

    step(large_relay, 1)

    @on(0)
    def _():
        step(give_turn)
        step(spread_same, hb, 0, 0, mc_s.at[0])

    step(large_finish, 1)

    @on(1)
    def _():
        pass_on(spread_far, h_mid, hb, 0, p)

    step(spread_own, hb, 0, 1)
    step(block_gates, 1)

    @on(0)
    def _():
        step(block_out, 1, h_late[0])
        pass_on(spread_near, h_late, hb, 0, 1)
        pass_on(spread_far, h_late, hb, 0, 1)
        step(spread_relay, hb, 0, 0)
        step(spread_finish, hb, 0, 0)
        step(grad_first, 0)
        step(spread_own, eb, 1, 1)
        step(block_backward, 1, e_first[0])
        pass_on(spread_near, e_first, eb, 1, 0)
        pass_on(spread_far, e_first, eb, 1, 0)
        pass_on(spread_far, h_mid, hb, 0, p)
        step(spread_relay, eb, 1, 1)
        step(spread_relay, hb, 0, 1)
        step(spread_finish, hb, 0, 1)
        step(grad_first, 1)

    @on(1)
    def _():
        step(spread_relay, hb, 0, 1)
        step(block_backward, 1, e_first[0])
        pass_on(spread_near, e_first, eb, 1, 1)
        pass_on(spread_far, e_first, eb, 1, 1)
        step(spread_same, eb, 1, 1, mc_s.at[0])
        step(spread_finish, hb, 0, 1)
        step(grad_first, 1)
        step(spread_relay, eb, 1, 1)
        step(spread_own, eb, 1, 0)
        step(block_backward, 0, e_last[0])
        pass_on(spread_near, e_last, eb, 1, 0)
        pass_on(spread_far, e_last, eb, 1, 0)
        step(spread_relay, eb, 1, 0)

    step(spread_finish, eb, 1, 1)
    step(grad_hidden, 1)
    step(grad_out, 1)
    step(scatter_send, 1, OUT, 0, MERGED + DIRECT)
    step(grad_in, 1)

    @on(0)
    def _():
        step(spread_relay, eb, 1, 0)

    step(scatter_send, 1, IN, 0, MERGED + DIRECT)

    @on(0)
    def _():
        step(spread_own, eb, 1, 0)
        step(block_backward, 0, ga)
        send(ga, ga, ga_s, ga_r, d, 1)

    @on(1)
    def _():
        step(spread_relay, hb, 0, 0)
        step(spread_finish, hb, 0, 0)
        step(grad_first, 0)

    step(spread_finish, eb, 1, 0)
    step(scatter_relay, 1, OUT, 0)
    step(grad_hidden, 0)
    step(grad_out, 0)
    step(scatter_send, 0, OUT, 0, MERGED)
    step(scatter_relay, 1, IN, 0)
    step(grad_in, 0)
    step(scatter_send, 0, IN, 0, MERGED)
    step(scatter_send, 0, OUT, 0, DIRECT)
    step(scatter_turn, 1, OUT)
    step(scatter_turn, 1, IN)
    step(scatter_send, 0, IN, 0, DIRECT)
    step(scatter_relay, 0, OUT, 0)
    step(scatter_relay, 0, IN, 0)
    step(scatter_relay, 1, OUT, 1)
    step(scatter_relay, 1, IN, 1)

    @on(1)
    def _():
        wait_recv(ga, ga_r)

    gact[...] = ga[...]
    step(scatter_turn, 0, OUT)
    step(scatter_turn, 0, IN)
    step(scatter_last, 1)
    step(scatter_relay, 0, OUT, 1)
    step(scatter_relay, 0, IN, 1)
    step(scatter_finish, 1)
    step(scatter_last, 0)
    step(scatter_finish, 0)

    for v in BLOCKS:
        for k in (X, Y, Z):
            wait_send(wts[k].at[v, 0, 0, pl.ds(0, 3)], ag_s.at[v, k, 0])
            wait_send(wts[k].at[v, 0, pl.ds(0, 3)], ag_s.at[v, k, 1])
            wait_send(wts[k].at[v, pl.ds(0, 3)], ag_s.at[v, k, LARGE])
        for colour in COLOURS:
            for which in HALVES:
                for st in HALVES:
                    wait_send(RECV[st][which][colour].at[v], rs_s.at[st, v, colour, which])
        wait_send(r3.at[v], r3_s.at[v])
        wait_send(hb.at[v, 0], rl_s.at[0, v])
        wait_send(hb.at[v, 0], rl_s.at[1, v])
    wait_send(hb.at[0, pl.ds(0, 2)], mc_s.at[0])
    wait_send(hb.at[0, pl.ds(0, 3)], mc_s.at[1])
    wait_send(hb.at[0, pl.ds(0, 3)], mc_s.at[3])

    @pl.when(p == 0)
    def _():
        wait_send(hb.at[0, pl.ds(0, 3)], mc_s.at[2])
        wait_send(ga, ga_s)

    @pl.when(p == 1)
    def _():
        wait_send(hb.at[0, pl.ds(0, 3)], mc_s.at[4])


def hand_on(*refs):
    srcs, dsts, bufs = refs[:NA], refs[NA:2 * NA], refs[2 * NA:3 * NA]
    sem_in, sem_out = refs[3 * NA:]
    into = [pltpu.make_async_copy(srcs[i], bufs[i], sem_in.at[i]) for i in QUARTERS]
    onto = [pltpu.make_async_copy(bufs[i], dsts[i], sem_out.at[i]) for i in QUARTERS]
    for copy in into:
        copy.start()
    for i in QUARTERS:
        into[i].wait()
        onto[i].start()
    for copy in onto:
        copy.wait()


def solution(mesh):
    act_spec = P(None, "data", None, None)
    w_spec = P(None, "stage", "data", None)

    def body(act_in, cot_out, w_gate, w_in, w_out):
        shape = act_in.shape
        dm, fd = shape[3], w_gate.shape[3]
        rows = shape[0] * shape[1] * shape[2]
        dr, fr, fs = dm // NL, fd // NL, fd // NA
        pf = fs // NA
        vmem = pltpu.VMEM
        dma = pltpu.SemaphoreType.DMA
        n2, n3, na = NB, len(RING), NA
        ring = (na, na)
        scratch = [
            vmem((n2, na, *ring, dr, fd), BF), vmem((n2, na, *ring, dr, fd), BF), vmem((n2, na, *ring, fr, dm), BF),
            vmem((n2, na, rows, dm), BF), vmem((n2, na, rows, dm), BF), vmem((na, rows, dm), BF), vmem((rows, dm), BF),
            vmem((n2, na, rows, dm), BF),
            vmem((n2, rows, fd), F32), vmem((n2, rows, fd), F32),
            vmem((n2, na, rows, fs), F32), vmem((n2, na, rows, fs), F32),
            vmem((n2, na, rows, fs), BF),
            vmem((rows, fd), BF), vmem((rows, fd), BF), vmem((rows, fd), BF),
            vmem((na, rows, fs), BF), vmem((na, rows, fs), BF),
            vmem((rows, dm), F32),
            vmem((dm, fs), BF), vmem((dm, fs), BF), vmem((fs, dm), BF),
            vmem((n2, n2, na, *ring, dr, fs), F32), vmem((n2, *ring, fr, dm), F32),
            vmem((n2, na, n2, dr, fs), F32), vmem((n2, n3, n2, dr, fs), F32),
            dma((n2, na)), dma((n2, n3, n3)), dma((n2, n3, n2, 6)), dma((n2, n3, n3 * na)), dma((5,)), dma((n2, n2, 5)), dma((n2, n2)), dma, dma,
            dma((n2, n2, n2, n2)), dma((n2, n2, n2, n2, 6)), dma((n2,)), dma((n2, n3)), pltpu.SemaphoreType.REGULAR,
            *(vmem((n2, 6, *lead, width), F32)
              for lead_in, lead_out in (((*ring, dr), (n2, fr)), ((na, dr), (fr // n2,)))
              for lead, total in ((lead_in, fs), (lead_out, dm))
              for width in (total - pf, pf)),
        ]
        hbm = pl.BlockSpec(memory_space=pl.ANY)
        whole = pl.BlockSpec(memory_space=pltpu.VMEM)
        out = pl.pallas_call(
            kernel,
            out_shape=(
                jax.ShapeDtypeStruct((rows, dm), BF),
                jax.ShapeDtypeStruct((2, dr, fd), F32), jax.ShapeDtypeStruct((2, dr, fd), F32),
                jax.ShapeDtypeStruct((2, fr, dm), F32),
            ),
            in_specs=[hbm] * 5,
            out_specs=(whole,) * NA,
            scratch_shapes=scratch,
            compiler_params=pltpu.CompilerParams(collective_id=0, has_side_effects=True, vmem_limit_bytes=67043328),
            name="train_step",
        )(act_in.reshape(rows, dm), cot_out.reshape(rows, dm), w_gate[:, 0], w_in[:, 0], w_out[:, 0])
        grad_act, grad_gate, grad_lin, grad_proj = pl.pallas_call(
            hand_on, out_shape=tuple(jax.ShapeDtypeStruct(a.shape, a.dtype) for a in out), in_specs=[hbm] * NA, out_specs=(hbm,) * NA,
            scratch_shapes=[*(vmem(a.shape, a.dtype) for a in out), dma((NA,)), dma((NA,))], name="hand_on",
        )(*out)
        return grad_act.reshape(shape), grad_gate[:, None], grad_lin[:, None], grad_proj[:, None]

    return jax.shard_map(body, mesh=mesh, in_specs=(act_spec, act_spec, w_spec, w_spec, w_spec),
                         out_specs=(act_spec, w_spec, w_spec, w_spec), check_vma=False)
```

time: 3850 us -> 125 us (0.03)
  waiting for transfers between devices: 1410 us -> 0 us
  matrix products: 1220 us -> 0 us
  local copies, waits for them, and re-layouts: 955 us -> 0 us
  other arithmetic: 125 us -> 0 us
  Pallas kernels: 0 us -> 124 us
  loops' own time: 89.2 us -> 0 us
    dot_general x650 -> x0, matrix products: 1220 us -> none  [the longest x195 354 us: contract_cols(): lax.dot_general(left, right, (((1,), (1,)), ((), ())), preferred_element_...]
    reduce_scatter x3 -> x0, waiting for transfers between devices: 1110 us -> none  [the longest x1 375 us: body(): lax.psum_scatter(carry_out[3], 'data', scatter_dimension=1, tiled=True)]
    dynamic_slice x261 -> x0, local copies, waits for them, and re-layouts: 472 us -> none  [the longest x130 398 us: pick_at(): return lax.dynamic_index_in_dim(stack, index, keepdims=False)]
    while x780 -> x0, local copies, waits for them, and re-layouts: 468 us -> none
    all_gather x3 -> x0, waiting for transfers between devices: 211 us -> none  [the longest x1 72.7 us: body(): gate_full = lax.all_gather(w_gate[:, 0], 'data', axis=1, tiled=True)]
    pallas_call x0 -> x2, Pallas kernels: none -> 124 us  [the longest x1 122 us: body(): pl.pallas_call(kernel, out_shape=(jax.ShapeDtypeStruct((rows, dm), BF), j...]
    another operation x2 -> x0, loops' own time: 89.2 us -> none  [the longest x1 50.5 us: body(): lax.scan(bwd_tick, (zero_rows, zero_up, zero_up, zero_down), tick_ids)]
    ppermute x130 -> x0, waiting for transfers between devices: 65.8 us -> none  [the longest x65 65.6 us: fwd_tick(): return (lax.ppermute(layer_out, 'stage', fwd_perm), layer_in)]
  transfers between devices with their start and end apart: 137 -> 0, of which waited for: 72 -> 0; matrix products, arithmetic and copies ran while one was open for 18% -> 0% of each run, Pallas kernels for 0% -> 0%
where the time goes in v1:
time: 125 us; the launch traced here: 124 us
  Pallas kernels  124 us (99%)
    pallas_call x1, Pallas kernels, body(): pl.pallas_call(kernel, out_shape=(jax.ShapeDtypeStruct((rows, dm), BF), j...  122 us

profile of v1, /device:TPU:0, one launch (start us, length us, event | category | flops | bytes accessed | tf_op | source)
XLA Modules:
  0.0 124.5 jit_solution(8380221118944086603)
XLA Ops:
  0.6 121.8 %train_step.1 = (bf16[256,512]{1,0:T(8,128)(2,1)}, f32[2,8,2048]{2,1,0:T(8,128)}, f32[2,8,2048]{2,1,0:T(8,128)}, f32[2,32,512]{2,1,0:T(8,128)}) custom-call(bf16[256,512]{1,0:T(8,128)(2,1)} %bitcast.17, bf16[256,512]{1,0:T(8,128)(2,1)} %bitcast.18, bf16[2,8,2048]{2,1,0:T(8,128)(2,1)} %bitcast.19, bf16[2,8,2048]{2,1,0:T(8,128)(2,1)} %bitcast.20, ...), custom_call_target="tpu_custom_call" | custom-call | tf_op jit(solution)/shard_map/train_step/pallas_call | solution.py:648
  122.4 1.8 %hand_on.1 = (bf16[256,512]{1,0:T(8,128)(2,1)}, f32[2,8,2048]{2,1,0:T(8,128)}, f32[2,8,2048]{2,1,0:T(8,128)}, f32[2,32,512]{2,1,0:T(8,128)}) custom-call(bf16[256,512]{1,0:T(8,128)(2,1)} %get-tuple-element.12.refs_0_, f32[2,8,2048]{2,1,0:T(8,128)} %get-tuple-element.13.refs_1_, f32[2,8,2048]{2,1,0:T(8,128)} %get-tuple-element.14.refs_2_, ...), custom_call_target="tpu_custom_call" | custom-call | tf_op jit(solution)/shard_map/hand_on/pallas_call | solution.py:661

commit v2 on v1

--- a/solution.py
+++ b/solution.py
@@ -426,6 +426,15 @@
     ALL = UP + (MINUS, OPP), DOWN + (0, PLUS)
     for v in BLOCKS:
         step(small_send, v, 0)
+
+    @on(0)
+    def _():
+        step(spread_same, hb, 0, 0, mc_s.at[0])
+
+    @on(1)
+    def _():
+        step(spread_same, eb, 1, 1, mc_s.at[0])
+
     for v in BLOCKS:
         step(small_relay, v, 0)
     step(small_rest, 0, 0)
@@ -469,15 +478,22 @@
     @on(0)
     def _():
         step(give_turn)
-        step(spread_same, hb, 0, 0, mc_s.at[0])
+        step(spread_relay, hb, 0, 0)
 
     step(large_finish, 1)
 
     @on(1)
     def _():
+        step(give_turn)
+        step(spread_relay, eb, 1, 1)
         pass_on(spread_far, h_mid, hb, 0, p)
 
     step(spread_own, hb, 0, 1)
+
+    @on(1)
+    def _():
+        step(spread_relay, hb, 0, 1)
+
     step(block_gates, 1)
 
     @on(0)
@@ -485,39 +501,39 @@
         step(block_out, 1, h_late[0])
         pass_on(spread_near, h_late, hb, 0, 1)
         pass_on(spread_far, h_late, hb, 0, 1)
-        step(spread_relay, hb, 0, 0)
         step(spread_finish, hb, 0, 0)
         step(grad_first, 0)
+        step(take_turn)
+        pass_on(spread_far, h_mid, hb, 0, p)
+        step(spread_relay, hb, 0, 1)
         step(spread_own, eb, 1, 1)
         step(block_backward, 1, e_first[0])
         pass_on(spread_near, e_first, eb, 1, 0)
         pass_on(spread_far, e_first, eb, 1, 0)
-        pass_on(spread_far, h_mid, hb, 0, p)
         step(spread_relay, eb, 1, 1)
-        step(spread_relay, hb, 0, 1)
         step(spread_finish, hb, 0, 1)
         step(grad_first, 1)
 
     @on(1)
     def _():
-        step(spread_relay, hb, 0, 1)
         step(block_backward, 1, e_first[0])
         pass_on(spread_near, e_first, eb, 1, 1)
         pass_on(spread_far, e_first, eb, 1, 1)
-        step(spread_same, eb, 1, 1, mc_s.at[0])
         step(spread_finish, hb, 0, 1)
         step(grad_first, 1)
-        step(spread_relay, eb, 1, 1)
+
+    step(spread_finish, eb, 1, 1)
+    step(grad_hidden, 1)
+    step(grad_out, 1)
+    step(scatter_send, 1, OUT, 0, MERGED + DIRECT)
+
+    @on(1)
+    def _():
         step(spread_own, eb, 1, 0)
         step(block_backward, 0, e_last[0])
         pass_on(spread_near, e_last, eb, 1, 0)
         pass_on(spread_far, e_last, eb, 1, 0)
-        step(spread_relay, eb, 1, 0)
-
-    step(spread_finish, eb, 1, 1)
-    step(grad_hidden, 1)
-    step(grad_out, 1)
-    step(scatter_send, 1, OUT, 0, MERGED + DIRECT)
+
     step(grad_in, 1)
 
     @on(0)
@@ -535,11 +551,12 @@
     @on(1)
     def _():
         step(spread_relay, hb, 0, 0)
+        step(spread_relay, eb, 1, 0)
         step(spread_finish, hb, 0, 0)
         step(grad_first, 0)
 
+    step(scatter_relay, 1, OUT, 0)
     step(spread_finish, eb, 1, 0)
-    step(scatter_relay, 1, OUT, 0)
     step(grad_hidden, 0)
     step(grad_out, 0)
     step(scatter_send, 0, OUT, 0, MERGED)
@@ -548,12 +565,11 @@
     step(scatter_send, 0, IN, 0, MERGED)
     step(scatter_send, 0, OUT, 0, DIRECT)
     step(scatter_turn, 1, OUT)
-    step(scatter_turn, 1, IN)
     step(scatter_send, 0, IN, 0, DIRECT)
     step(scatter_relay, 0, OUT, 0)
+    step(scatter_turn, 1, IN)
     step(scatter_relay, 0, IN, 0)
     step(scatter_relay, 1, OUT, 1)
-    step(scatter_relay, 1, IN, 1)
 
     @on(1)
     def _():
@@ -561,6 +577,7 @@
 
     gact[...] = ga[...]
     step(scatter_turn, 0, OUT)
+    step(scatter_relay, 1, IN, 1)
     step(scatter_turn, 0, IN)
     step(scatter_last, 1)
     step(scatter_relay, 0, OUT, 1)

time: 125 us -> 120 us (0.960)
  Pallas kernels: 124 us -> 119 us
    pallas_call x1, Pallas kernels: 122 us -> 118 us  [body(): pl.pallas_call(kernel, out_shape=(jax.ShapeDtypeStruct((rows, dm), BF), j...]
where the time goes in v2:
time: 120 us
  Pallas kernels  119 us (99%)
    pallas_call x1, Pallas kernels, body(): pl.pallas_call(kernel, out_shape=(jax.ShapeDtypeStruct((rows, dm), BF), j...  118 us

profile of v2, /device:TPU:0, one launch (start us, length us, event | category | flops | bytes accessed | tf_op | source)
XLA Modules:
  0.0 120.2 jit_solution(9178627707581129691)
XLA Ops:
  0.6 117.6 %train_step.1 = (bf16[256,512]{1,0:T(8,128)(2,1)}, f32[2,8,2048]{2,1,0:T(8,128)}, f32[2,8,2048]{2,1,0:T(8,128)}, f32[2,32,512]{2,1,0:T(8,128)}) custom-call(bf16[256,512]{1,0:T(8,128)(2,1)} %bitcast.17, bf16[256,512]{1,0:T(8,128)(2,1)} %bitcast.18, bf16[2,8,2048]{2,1,0:T(8,128)(2,1)} %bitcast.19, bf16[2,8,2048]{2,1,0:T(8,128)(2,1)} %bitcast.20, ...), custom_call_target="tpu_custom_call" | custom-call | tf_op jit(solution)/shard_map/train_step/pallas_call | solution.py:665
  118.2 1.8 %hand_on.1 = (bf16[256,512]{1,0:T(8,128)(2,1)}, f32[2,8,2048]{2,1,0:T(8,128)}, f32[2,8,2048]{2,1,0:T(8,128)}, f32[2,32,512]{2,1,0:T(8,128)}) custom-call(bf16[256,512]{1,0:T(8,128)(2,1)} %get-tuple-element.12.refs_0_, f32[2,8,2048]{2,1,0:T(8,128)} %get-tuple-element.13.refs_1_, f32[2,8,2048]{2,1,0:T(8,128)} %get-tuple-element.14.refs_2_, ...), custom_call_target="tpu_custom_call" | custom-call | tf_op jit(solution)/shard_map/hand_on/pallas_call | solution.py:678

commit v3 on v2

--- a/solution.py
+++ b/solution.py
@@ -366,7 +366,7 @@
                 wait_recv(recv.at[v, slot - 4], rs_r.at[st, v, colour, which, slot - 4])
                 ref = view(which, st, v, colour, rot(q, c), half)
                 ref[...] = ref[...] + recv[v, slot - 4]
-        scatter_send(v, which, st, RELAYED)
+        scatter_send(v, which, st, RELAYED + DIRECT)
 
     def scatter_sum(v, which, st):
         for colour in COLOURS:
@@ -381,7 +381,7 @@
 
     def scatter_turn(v, which):
         scatter_sum(v, which, 0)
-        scatter_send(v, which, 1, MERGED + DIRECT)
+        scatter_send(v, which, 1, MERGED)
 
     def scatter_last(v):
         scatter_sum(v, OUT, 1)
@@ -462,17 +462,13 @@
 
     @on(1)
     def _():
+        step(take_turn)
+        step(large_send, 1, *ALL)
         step(spread_own, hb, 0, 0)
 
     step(block_gates, 0)
     step(block_out, 0, h_mid[0])
     pass_on(spread_near, h_mid, hb, 0, p)
-
-    @on(1)
-    def _():
-        step(take_turn)
-        step(large_send, 1, *ALL)
-
     step(large_relay, 1)
 
     @on(0)
@@ -484,16 +480,10 @@
 
     @on(1)
     def _():
-        step(give_turn)
-        step(spread_relay, eb, 1, 1)
+        step(spread_relay, hb, 0, 1)
         pass_on(spread_far, h_mid, hb, 0, p)
 
     step(spread_own, hb, 0, 1)
-
-    @on(1)
-    def _():
-        step(spread_relay, hb, 0, 1)
-
     step(block_gates, 1)
 
     @on(0)
@@ -503,19 +493,19 @@
         pass_on(spread_far, h_late, hb, 0, 1)
         step(spread_finish, hb, 0, 0)
         step(grad_first, 0)
-        step(take_turn)
-        pass_on(spread_far, h_mid, hb, 0, p)
         step(spread_relay, hb, 0, 1)
         step(spread_own, eb, 1, 1)
         step(block_backward, 1, e_first[0])
         pass_on(spread_near, e_first, eb, 1, 0)
         pass_on(spread_far, e_first, eb, 1, 0)
+        pass_on(spread_far, h_mid, hb, 0, p)
         step(spread_relay, eb, 1, 1)
         step(spread_finish, hb, 0, 1)
         step(grad_first, 1)
 
     @on(1)
     def _():
+        step(spread_relay, eb, 1, 1)
         step(block_backward, 1, e_first[0])
         pass_on(spread_near, e_first, eb, 1, 1)
         pass_on(spread_far, e_first, eb, 1, 1)
@@ -525,7 +515,7 @@
     step(spread_finish, eb, 1, 1)
     step(grad_hidden, 1)
     step(grad_out, 1)
-    step(scatter_send, 1, OUT, 0, MERGED + DIRECT)
+    step(scatter_send, 1, OUT, 0, MERGED)
 
     @on(1)
     def _():
@@ -540,13 +530,15 @@
     def _():
         step(spread_relay, eb, 1, 0)
 
-    step(scatter_send, 1, IN, 0, MERGED + DIRECT)
+    step(scatter_send, 1, IN, 0, MERGED)
 
     @on(0)
     def _():
         step(spread_own, eb, 1, 0)
         step(block_backward, 0, ga)
         send(ga, ga, ga_s, ga_r, d, 1)
+
+    step(scatter_relay, 1, OUT, 0)
 
     @on(1)
     def _():
@@ -555,20 +547,18 @@
         step(spread_finish, hb, 0, 0)
         step(grad_first, 0)
 
-    step(scatter_relay, 1, OUT, 0)
+    step(scatter_relay, 1, IN, 0)
     step(spread_finish, eb, 1, 0)
     step(grad_hidden, 0)
     step(grad_out, 0)
     step(scatter_send, 0, OUT, 0, MERGED)
-    step(scatter_relay, 1, IN, 0)
     step(grad_in, 0)
     step(scatter_send, 0, IN, 0, MERGED)
-    step(scatter_send, 0, OUT, 0, DIRECT)
     step(scatter_turn, 1, OUT)
-    step(scatter_send, 0, IN, 0, DIRECT)
     step(scatter_relay, 0, OUT, 0)
+    step(scatter_relay, 0, IN, 0)
     step(scatter_turn, 1, IN)
-    step(scatter_relay, 0, IN, 0)
+    step(scatter_turn, 0, OUT)
     step(scatter_relay, 1, OUT, 1)
 
     @on(1)
@@ -576,14 +566,13 @@
         wait_recv(ga, ga_r)
 
     gact[...] = ga[...]
-    step(scatter_turn, 0, OUT)
+    step(scatter_turn, 0, IN)
     step(scatter_relay, 1, IN, 1)
-    step(scatter_turn, 0, IN)
-    step(scatter_last, 1)
     step(scatter_relay, 0, OUT, 1)
     step(scatter_relay, 0, IN, 1)
+    step(scatter_last, 1)
+    step(scatter_last, 0)
     step(scatter_finish, 1)
-    step(scatter_last, 0)
     step(scatter_finish, 0)
 
     for v in BLOCKS:

time: 120 us -> 122 us (1.017)
  Pallas kernels: 119 us -> 121 us
    pallas_call x1, Pallas kernels: 118 us -> 120 us  [body(): pl.pallas_call(kernel, out_shape=(jax.ShapeDtypeStruct((rows, dm), BF), j...]
where the time goes in v3:
time: 122 us
  Pallas kernels  121 us (99%)
    pallas_call x1, Pallas kernels, body(): pl.pallas_call(kernel, out_shape=(jax.ShapeDtypeStruct((rows, dm), BF), j...  120 us

profile of v3, /device:TPU:0, one launch (start us, length us, event | category | flops | bytes accessed | tf_op | source)
XLA Modules:
  0.0 122.2 jit_solution(11712249825858849781)
XLA Ops:
  0.6 119.6 %train_step.1 = (bf16[256,512]{1,0:T(8,128)(2,1)}, f32[2,8,2048]{2,1,0:T(8,128)}, f32[2,8,2048]{2,1,0:T(8,128)}, f32[2,32,512]{2,1,0:T(8,128)}) custom-call(bf16[256,512]{1,0:T(8,128)(2,1)} %bitcast.17, bf16[256,512]{1,0:T(8,128)(2,1)} %bitcast.18, bf16[2,8,2048]{2,1,0:T(8,128)(2,1)} %bitcast.19, bf16[2,8,2048]{2,1,0:T(8,128)(2,1)} %bitcast.20, ...), custom_call_target="tpu_custom_call" | custom-call | tf_op jit(solution)/shard_map/train_step/pallas_call | solution.py:654
  120.2 1.8 %hand_on.1 = (bf16[256,512]{1,0:T(8,128)(2,1)}, f32[2,8,2048]{2,1,0:T(8,128)}, f32[2,8,2048]{2,1,0:T(8,128)}, f32[2,32,512]{2,1,0:T(8,128)}) custom-call(bf16[256,512]{1,0:T(8,128)(2,1)} %get-tuple-element.12.refs_0_, f32[2,8,2048]{2,1,0:T(8,128)} %get-tuple-element.13.refs_1_, f32[2,8,2048]{2,1,0:T(8,128)} %get-tuple-element.14.refs_2_, ...), custom_call_target="tpu_custom_call" | custom-call | tf_op jit(solution)/shard_map/hand_on/pallas_call | solution.py:667

commit v4 on v2

--- a/solution.py
+++ b/solution.py
@@ -18,6 +18,7 @@
 OPP = RING[-1]
 PLUS, MINUS = RING[:-1]
 QUARTERS = range(NA)
+OWN = 0
 AXES = ((X, Y, Z), (Y, Z, X), (Z, X, Y))
 
 
@@ -88,11 +89,11 @@
 
     @pl.when(p == 0)
     def _():
-        pltpu.make_async_copy(act, hb.at[0, ja], lsem.at[0, 3]).start()
+        pltpu.make_async_copy(act, hb.at[0, OWN], lsem.at[0, 3]).start()
 
     @pl.when(p == 1)
     def _():
-        pltpu.make_async_copy(cot, eb.at[1, ja], lsem.at[0, 3]).start()
+        pltpu.make_async_copy(cot, eb.at[1, OWN], lsem.at[0, 3]).start()
 
     barrier = pltpu.get_barrier_semaphore()
     senders = [(peer(ax, delta), p) for ax in (X, Y, Z) for delta in RING]
@@ -105,11 +106,11 @@
 
     @pl.when(p == 0)
     def _():
-        pltpu.make_async_copy(act, hb.at[0, ja], lsem.at[0, 3]).wait()
+        pltpu.make_async_copy(act, hb.at[0, OWN], lsem.at[0, 3]).wait()
 
     @pl.when(p == 1)
     def _():
-        pltpu.make_async_copy(cot, eb.at[1, ja], lsem.at[0, 3]).wait()
+        pltpu.make_async_copy(cot, eb.at[1, OWN], lsem.at[0, 3]).wait()
 
     pl.semaphore_wait(barrier, len(senders))
 
@@ -190,32 +191,31 @@
                 wait_recv(row(v, k, rot(coord[AXES[k][LARGE]], OPP), r), lg_r.at[v, k, 2 * NA + r])
 
     half_rows = rows // 2
+    BACK, AHEAD, FAR = 1, 2, 3
 
     def spread_near(src, buf, which, vd, ssem):
-        send(src, buf.at[vd, jb], ssem, mc_r.at[which, vd, 0], d, 1 - p)
+        send(src, buf.at[vd, OWN], ssem, mc_r.at[which, vd, OWN], d, 1 - p)
 
     def spread_far(src, buf, which, vd, ssem):
-        send(src, buf.at[vd, jb], ssem, mc_r.at[which, vd, 1], peer_b(1), 1 - p)
-        send(src, buf.at[vd, jb], ssem, mc_r.at[which, vd, 2], peer_b(-1), 1 - p)
+        send(src, buf.at[vd, BACK], ssem, mc_r.at[which, vd, BACK], peer_b(PLUS), 1 - p)
+        send(src, buf.at[vd, AHEAD], ssem, mc_r.at[which, vd, AHEAD], peer_b(MINUS), 1 - p)
 
     def spread_same(buf, which, v, ssem):
-        own = buf.at[v, ja]
-        send(own, own, ssem, mc_r.at[which, v, 1], peer_a(1), p)
-        send(own, own, ssem, mc_r.at[which, v, 2], peer_a(-1), p)
+        send(buf.at[v, OWN], buf.at[v, BACK], ssem, mc_r.at[which, v, BACK], peer_a(PLUS), p)
+        send(buf.at[v, OWN], buf.at[v, AHEAD], ssem, mc_r.at[which, v, AHEAD], peer_a(MINUS), p)
 
     def spread_relay(buf, which, v):
-        for half, delta in ((0, 1), (1, 3)):
-            slot = rot(ja, -delta)
-            wait_recv(buf.at[v, slot], mc_r.at[which, v, 1 + half])
-            ref = buf.at[v, slot, pl.ds(half * half_rows, half_rows)]
-            send(ref, ref, rl_s.at[which, v], mc_r.at[which, v, 3 + half], peer_a(delta), p)
+        for half, slot, delta in ((0, BACK, PLUS), (1, AHEAD, MINUS)):
+            wait_recv(buf.at[v, slot], mc_r.at[which, v, slot])
+            part = pl.ds(half * half_rows, half_rows)
+            send(buf.at[v, slot, part], buf.at[v, FAR, part], rl_s.at[which, v], mc_r.at[which, v, FAR + half], peer_a(delta), p)
 
     def spread_finish(buf, which, v):
         for half in HALVES:
-            wait_recv(buf.at[v, rot(ja, 2), pl.ds(half * half_rows, half_rows)], mc_r.at[which, v, 3 + half])
+            wait_recv(buf.at[v, FAR, pl.ds(half * half_rows, half_rows)], mc_r.at[which, v, FAR + half])
 
     def spread_own(buf, which, v):
-        wait_recv(buf.at[v, ja], mc_r.at[which, v, 0])
+        wait_recv(buf.at[v, OWN], mc_r.at[which, v, OWN])
 
     def gates(n, wgt, wlin):
         a, b = mm(n, wgt), mm(n, wlin)
@@ -224,7 +224,7 @@
         return (act_a * b).astype(BF), b * s * (1.0 + a * (1.0 - s)), act_a
 
     def block_gates(v):
-        h = hb[v, ja].astype(F32)
+        h = hb[v, OWN].astype(F32)
         n = (h * inv_rms(h)).astype(BF)
 
         def tile(i, carry):
@@ -243,10 +243,10 @@
         for i in HALVES:
             cols = pl.ds(i * half_dm, half_dm)
             out = mm(ub[...], wo[v, :, :, :, :, cols].reshape(fd, half_dm))
-            dst[:, cols] = (hb[v, ja, :, cols].astype(F32) + out).astype(BF)
+            dst[:, cols] = (hb[v, OWN, :, cols].astype(F32) + out).astype(BF)
 
     def block_backward(v, dst):
-        e = eb[v, ja]
+        e = eb[v, OWN]
 
         def tile(i, carry):
             cols = pl.ds(pl.multiple_of(i * fs, fs), fs)
@@ -261,7 +261,7 @@
             q = mm_nt(da[...], wg[v, pl.ds(2 * i, 2)].reshape(half_dm, fd))
             q += mm_nt(db[...], wi[v, pl.ds(2 * i, 2)].reshape(half_dm, fd))
             qs[:, pl.ds(i * half_dm, half_dm)] = q
-        h = hb[v, ja].astype(F32)
+        h = hb[v, OWN].astype(F32)
         r = inv_rms(h)
         hr = h * r
         q = qs[...]
@@ -272,59 +272,51 @@
         y = j + p * (i - j)
         return z, y
 
-    def grad_first(v):
-        for i in QUARTERS:
+    EARLY, LATE = range(FAR), range(FAR, NA)
+
+    def grad_first(v, slots):
+        for i in QUARTERS if OWN in slots else ():
             z, y = piece(ja, i)
             cols = pl.ds(pl.multiple_of((z * NA + y) * pf, pf), pf)
-            gs[:, pl.ds(i * pf, pf)] = wg[v, :, :, :, :, cols].reshape(dm, pf)
-            is_[:, pl.ds(i * pf, pf)] = wi[v, :, :, :, :, cols].reshape(dm, pf)
-
-        def tile(s, carry):
+            gs[v, :, pl.ds(i * pf, pf)] = wg[v, :, :, :, :, cols].reshape(dm, pf)
+            is_[v, :, pl.ds(i * pf, pf)] = wi[v, :, :, :, :, cols].reshape(dm, pf)
+        for s in slots:
             h = hb[v, s].astype(F32)
             n = (h * inv_rms(h)).astype(BF)
             ng[v, s] = n
-            u, t1, t2 = gates(n, gs[...], is_[...])
+            u, t1, t2 = gates(n, gs[v], is_[v])
             us[v, s] = u
             f1s[v, s] = t1
             f2s[v, s] = t2
-            return carry
-
-        lax.fori_loop(0, NA, tile, 0, unroll=True)
-
-    def grad_hidden(v):
-        for i in QUARTERS:
+
+    def grad_hidden(v, slots):
+        for i in QUARTERS if OWN in slots else ():
             z, y = piece(ja, i)
             os_[pl.ds(i * pf, pf), :] = wo[v, z, y].reshape(pf, dm)
-
-        def tile(s, carry):
+        for s in slots:
             t = mm_nt(eb[v, s], os_[...])
             das[s] = (t * f1s[v, s]).astype(BF)
             dbs[s] = (t * f2s[v, s]).astype(BF)
-            return carry
-
-        lax.fori_loop(0, NA, tile, 0, unroll=True)
-
-    def grad_out(v):
-        def tile(i, carry):
-            cols = pl.ds(pl.multiple_of(i * 2 * pf, 2 * pf), 2 * pf)
-            g = mm_tn(us[v, :, :, cols].reshape(NA * rows, 2 * pf), eb[v].reshape(NA * rows, dm))
-            gout[v, pl.ds(2 * i, 2)] = g.reshape(2, 4, fr, dm)
-            return carry
-
-        lax.fori_loop(0, 2, tile, 0, unroll=True)
-
-    def grad_in(v):
+
+    def rows_of(slots):
+        return pl.ds(slots[0], len(slots)), len(slots) * rows
+
+    def grad_out(v, slots):
+        some, count = rows_of(slots)
+        for i in HALVES:
+            cols, to = pl.ds(i * 2 * pf, 2 * pf), pl.ds(2 * i, 2)
+            g = mm_tn(us[v, some, :, cols].reshape(count, 2 * pf), eb[v, some].reshape(count, dm)).reshape(2, 4, fr, dm)
+            gout[v, to] = g if OWN in slots else gout[v, to] + g
+
+    def grad_in(v, slots):
+        some, count = rows_of(slots)
         for which, dref in enumerate((das, dbs)):
-
-            def tile(i, carry, which=which, dref=dref):
-                cols = pl.ds(pl.multiple_of(i * (dm // NA), dm // NA), dm // NA)
-                g = mm_tn(ng[v, :, :, cols].reshape(NA * rows, dm // NA), dref[...].reshape(NA * rows, fs)).reshape(4, 4, dr, fs)
-
+            for i in QUARTERS:
+                cols = pl.ds(i * (dm // NA), dm // NA)
+                g = mm_tn(ng[v, some, :, cols].reshape(count, dm // NA), dref[some].reshape(count, fs)).reshape(4, 4, dr, fs)
                 for y in QUARTERS:
-                    gin[v, which, y + p * (i - y), i + p * (y - i)] = g[y]
-                return carry
-
-            lax.fori_loop(0, NA, tile, 0, unroll=True)
+                    at = (v, which, y + p * (i - y), i + p * (y - i))
+                    gin[at] = g[y] if OWN in slots else gin[at] + g[y]
 
     IN, OUT = 0, 1
 
@@ -337,7 +329,7 @@
             cols = split(fs)[colour]
             b, x = (t, slice(None) if st == 0 else xc) if along_b else (slice(None) if st == 0 else jb, t)
             return gin.at[v, half, :, b, x, :, cols]
-        cols = split(dm)[colour]
+        cols = pl.ds(colour * (dm // 2), dm // 2)
         if st == 0:
             hs = pl.ds(2 * half, 2)
             return gout.at[v, t, hs, :, cols] if along_b else gout.at[v, hs, t, :, cols]
@@ -462,17 +454,13 @@
 
     @on(1)
     def _():
+        step(take_turn)
+        step(large_send, 1, *ALL)
         step(spread_own, hb, 0, 0)
 
     step(block_gates, 0)
     step(block_out, 0, h_mid[0])
     pass_on(spread_near, h_mid, hb, 0, p)
-
-    @on(1)
-    def _():
-        step(take_turn)
-        step(large_send, 1, *ALL)
-
     step(large_relay, 1)
 
     @on(0)
@@ -485,15 +473,10 @@
     @on(1)
     def _():
         step(give_turn)
-        step(spread_relay, eb, 1, 1)
+        step(spread_relay, hb, 0, 1)
         pass_on(spread_far, h_mid, hb, 0, p)
 
     step(spread_own, hb, 0, 1)
-
-    @on(1)
-    def _():
-        step(spread_relay, hb, 0, 1)
-
     step(block_gates, 1)
 
     @on(0)
@@ -502,7 +485,8 @@
         pass_on(spread_near, h_late, hb, 0, 1)
         pass_on(spread_far, h_late, hb, 0, 1)
         step(spread_finish, hb, 0, 0)
-        step(grad_first, 0)
+        step(grad_first, 0, EARLY)
+        step(grad_first, 0, LATE)
         step(take_turn)
         pass_on(spread_far, h_mid, hb, 0, p)
         step(spread_relay, hb, 0, 1)
@@ -510,59 +494,73 @@
         step(block_backward, 1, e_first[0])
         pass_on(spread_near, e_first, eb, 1, 0)
         pass_on(spread_far, e_first, eb, 1, 0)
+
+    @on(1)
+    def _():
         step(spread_relay, eb, 1, 1)
-        step(spread_finish, hb, 0, 1)
-        step(grad_first, 1)
-
-    @on(1)
-    def _():
         step(block_backward, 1, e_first[0])
         pass_on(spread_near, e_first, eb, 1, 1)
         pass_on(spread_far, e_first, eb, 1, 1)
-        step(spread_finish, hb, 0, 1)
-        step(grad_first, 1)
+
+    step(grad_first, 1, EARLY)
+
+    @on(0)
+    def _():
+        step(spread_relay, eb, 1, 1)
+
+    step(grad_hidden, 1, EARLY)
+    step(grad_out, 1, EARLY)
+
+    @on(0)
+    def _():
+        step(grad_in, 1, EARLY)
+
+    step(spread_finish, hb, 0, 1)
+    step(grad_first, 1, LATE)
+
+    @on(0)
+    def _():
+        step(spread_own, eb, 1, 0)
+        step(block_backward, 0, ga)
+        send(ga, ga, ga_s, ga_r, d, 1)
 
     step(spread_finish, eb, 1, 1)
-    step(grad_hidden, 1)
-    step(grad_out, 1)
-    step(scatter_send, 1, OUT, 0, MERGED + DIRECT)
+    step(grad_hidden, 1, LATE)
+    step(grad_out, 1, LATE)
+    step(scatter_send, 1, OUT, 0, MERGED)
 
     @on(1)
     def _():
+        step(spread_relay, hb, 0, 0)
+        step(grad_first, 0, EARLY)
         step(spread_own, eb, 1, 0)
         step(block_backward, 0, e_last[0])
         pass_on(spread_near, e_last, eb, 1, 0)
         pass_on(spread_far, e_last, eb, 1, 0)
-
-    step(grad_in, 1)
-
-    @on(0)
-    def _():
-        step(spread_relay, eb, 1, 0)
-
-    step(scatter_send, 1, IN, 0, MERGED + DIRECT)
-
-    @on(0)
-    def _():
-        step(spread_own, eb, 1, 0)
-        step(block_backward, 0, ga)
-        send(ga, ga, ga_s, ga_r, d, 1)
+        step(grad_in, 1, EARLY)
+
+    step(grad_in, 1, LATE)
+    step(scatter_send, 1, IN, 0, MERGED)
+    step(scatter_send, 1, OUT, 0, DIRECT)
+    step(spread_relay, eb, 1, 0)
 
     @on(1)
     def _():
-        step(spread_relay, hb, 0, 0)
-        step(spread_relay, eb, 1, 0)
         step(spread_finish, hb, 0, 0)
-        step(grad_first, 0)
-
+        step(grad_first, 0, LATE)
+
+    step(grad_hidden, 0, EARLY)
+    step(scatter_send, 1, IN, 0, DIRECT)
+    step(grad_out, 0, EARLY)
     step(scatter_relay, 1, OUT, 0)
+    step(grad_in, 0, EARLY)
     step(spread_finish, eb, 1, 0)
-    step(grad_hidden, 0)
-    step(grad_out, 0)
+    step(grad_hidden, 0, LATE)
+    step(grad_out, 0, LATE)
     step(scatter_send, 0, OUT, 0, MERGED)
+    step(grad_in, 0, LATE)
+    step(scatter_send, 0, IN, 0, MERGED)
     step(scatter_relay, 1, IN, 0)
-    step(grad_in, 0)
-    step(scatter_send, 0, IN, 0, MERGED)
     step(scatter_send, 0, OUT, 0, DIRECT)
     step(scatter_turn, 1, OUT)
     step(scatter_send, 0, IN, 0, DIRECT)
@@ -579,11 +577,11 @@
     step(scatter_turn, 0, OUT)
     step(scatter_relay, 1, IN, 1)
     step(scatter_turn, 0, IN)
+    step(scatter_relay, 0, OUT, 1)
     step(scatter_last, 1)
-    step(scatter_relay, 0, OUT, 1)
     step(scatter_relay, 0, IN, 1)
+    step(scatter_last, 0)
     step(scatter_finish, 1)
-    step(scatter_last, 0)
     step(scatter_finish, 0)
 
     for v in BLOCKS:
@@ -650,15 +648,14 @@
             vmem((rows, fd), BF), vmem((rows, fd), BF), vmem((rows, fd), BF),
             vmem((na, rows, fs), BF), vmem((na, rows, fs), BF),
             vmem((rows, dm), F32),
-            vmem((dm, fs), BF), vmem((dm, fs), BF), vmem((fs, dm), BF),
+            vmem((n2, dm, fs), BF), vmem((n2, dm, fs), BF), vmem((fs, dm), BF),
             vmem((n2, n2, na, *ring, dr, fs), F32), vmem((n2, *ring, fr, dm), F32),
             vmem((n2, na, n2, dr, fs), F32), vmem((n2, n3, n2, dr, fs), F32),
             dma((n2, na)), dma((n2, n3, n3)), dma((n2, n3, n2, 6)), dma((n2, n3, n3 * na)), dma((5,)), dma((n2, n2, 5)), dma((n2, n2)), dma, dma,
             dma((n2, n2, n2, n2)), dma((n2, n2, n2, n2, 6)), dma((n2,)), dma((n2, n3)), pltpu.SemaphoreType.REGULAR,
             *(vmem((n2, 6, *lead, width), F32)
               for lead_in, lead_out in (((*ring, dr), (n2, fr)), ((na, dr), (fr // n2,)))
-              for lead, total in ((lead_in, fs), (lead_out, dm))
-              for width in (total - pf, pf)),
+              for lead, width in ((lead_in, fs - pf), (lead_in, pf), (lead_out, dm // n2), (lead_out, dm // n2))),
         ]
         hbm = pl.BlockSpec(memory_space=pl.ANY)
         whole = pl.BlockSpec(memory_space=pltpu.VMEM)

time: 120 us -> 117 us (0.975)
  Pallas kernels: 119 us -> 116 us
    pallas_call x1, Pallas kernels: 118 us -> 115 us  [body(): pl.pallas_call(kernel, out_shape=(jax.ShapeDtypeStruct((rows, dm), BF), j...]
where the time goes in v4:
time: 117 us
  Pallas kernels  116 us (99%)
    pallas_call x1, Pallas kernels, body(): pl.pallas_call(kernel, out_shape=(jax.ShapeDtypeStruct((rows, dm), BF), j...  115 us

profile of v4, /device:TPU:0, one launch (start us, length us, event | category | flops | bytes accessed | tf_op | source)
XLA Modules:
  0.0 117.3 jit_solution(10874394383815089814)
XLA Ops:
  0.6 114.6 %train_step.1 = (bf16[256,512]{1,0:T(8,128)(2,1)}, f32[2,8,2048]{2,1,0:T(8,128)}, f32[2,8,2048]{2,1,0:T(8,128)}, f32[2,32,512]{2,1,0:T(8,128)}) custom-call(bf16[256,512]{1,0:T(8,128)(2,1)} %bitcast.17, bf16[256,512]{1,0:T(8,128)(2,1)} %bitcast.18, bf16[2,8,2048]{2,1,0:T(8,128)(2,1)} %bitcast.19, bf16[2,8,2048]{2,1,0:T(8,128)(2,1)} %bitcast.20, ...), custom_call_target="tpu_custom_call" | custom-call | tf_op jit(solution)/shard_map/train_step/pallas_call | solution.py:662
  115.2 1.8 %hand_on.1 = (bf16[256,512]{1,0:T(8,128)(2,1)}, f32[2,8,2048]{2,1,0:T(8,128)}, f32[2,8,2048]{2,1,0:T(8,128)}, f32[2,32,512]{2,1,0:T(8,128)}) custom-call(bf16[256,512]{1,0:T(8,128)(2,1)} %get-tuple-element.12.refs_0_, f32[2,8,2048]{2,1,0:T(8,128)} %get-tuple-element.13.refs_1_, f32[2,8,2048]{2,1,0:T(8,128)} %get-tuple-element.14.refs_2_, ...), custom_call_target="tpu_custom_call" | custom-call | tf_op jit(solution)/shard_map/hand_on/pallas_call | solution.py:675

commit v5 on v4

--- a/solution.py
+++ b/solution.py
@@ -381,7 +381,7 @@
         scatter_sum(v, IN, 1)
         for which in HALVES:
             fin[v, :, which] = gin[v, which, :, jb, xc]
-        for delta in RING:
+        for delta in (OPP, PLUS, MINUS):
             send(fin.at[v, rot(ja, delta)], r3.at[v, delta - 1], r3_s.at[v], r3_r.at[v, delta - 1], peer_a(delta), p)
 
     def scatter_finish(v):
@@ -473,7 +473,6 @@
     @on(1)
     def _():
         step(give_turn)
-        step(spread_relay, hb, 0, 1)
         pass_on(spread_far, h_mid, hb, 0, p)
 
     step(spread_own, hb, 0, 1)
@@ -489,14 +488,15 @@
         step(grad_first, 0, LATE)
         step(take_turn)
         pass_on(spread_far, h_mid, hb, 0, p)
-        step(spread_relay, hb, 0, 1)
         step(spread_own, eb, 1, 1)
         step(block_backward, 1, e_first[0])
         pass_on(spread_near, e_first, eb, 1, 0)
         pass_on(spread_far, e_first, eb, 1, 0)
-
-    @on(1)
-    def _():
+        step(spread_relay, hb, 0, 1)
+
+    @on(1)
+    def _():
+        step(spread_relay, hb, 0, 1)
         step(spread_relay, eb, 1, 1)
         step(block_backward, 1, e_first[0])
         pass_on(spread_near, e_first, eb, 1, 1)
@@ -508,6 +508,10 @@
     def _():
         step(spread_relay, eb, 1, 1)
 
+    @on(1)
+    def _():
+        step(spread_relay, hb, 0, 0)
+
     step(grad_hidden, 1, EARLY)
     step(grad_out, 1, EARLY)
 
@@ -517,13 +521,6 @@
 
     step(spread_finish, hb, 0, 1)
     step(grad_first, 1, LATE)
-
-    @on(0)
-    def _():
-        step(spread_own, eb, 1, 0)
-        step(block_backward, 0, ga)
-        send(ga, ga, ga_s, ga_r, d, 1)
-
     step(spread_finish, eb, 1, 1)
     step(grad_hidden, 1, LATE)
     step(grad_out, 1, LATE)
@@ -531,8 +528,6 @@
 
     @on(1)
     def _():
-        step(spread_relay, hb, 0, 0)
-        step(grad_first, 0, EARLY)
         step(spread_own, eb, 1, 0)
         step(block_backward, 0, e_last[0])
         pass_on(spread_near, e_last, eb, 1, 0)
@@ -541,6 +536,17 @@
 
     step(grad_in, 1, LATE)
     step(scatter_send, 1, IN, 0, MERGED)
+
+    @on(0)
+    def _():
+        step(spread_own, eb, 1, 0)
+        step(block_backward, 0, ga)
+        send(ga, ga, ga_s, ga_r, d, 1)
+
+    @on(1)
+    def _():
+        step(grad_first, 0, EARLY)
+
     step(scatter_send, 1, OUT, 0, DIRECT)
     step(spread_relay, eb, 1, 0)
 
@@ -611,16 +617,10 @@
 
 
 def hand_on(*refs):
-    srcs, dsts, bufs = refs[:NA], refs[NA:2 * NA], refs[2 * NA:3 * NA]
-    sem_in, sem_out = refs[3 * NA:]
-    into = [pltpu.make_async_copy(srcs[i], bufs[i], sem_in.at[i]) for i in QUARTERS]
-    onto = [pltpu.make_async_copy(bufs[i], dsts[i], sem_out.at[i]) for i in QUARTERS]
-    for copy in into:
+    copies = [pltpu.make_async_copy(refs[i], refs[NA + i], refs[-1].at[i]) for i in QUARTERS]
+    for copy in copies:
         copy.start()
-    for i in QUARTERS:
-        into[i].wait()
-        onto[i].start()
-    for copy in onto:
+    for copy in copies:
         copy.wait()
 
 
@@ -662,20 +662,18 @@
         out = pl.pallas_call(
             kernel,
             out_shape=(
-                jax.ShapeDtypeStruct((rows, dm), BF),
-                jax.ShapeDtypeStruct((2, dr, fd), F32), jax.ShapeDtypeStruct((2, dr, fd), F32),
-                jax.ShapeDtypeStruct((2, fr, dm), F32),
+                vmem((rows, dm), BF), vmem((n2, dr, fd), F32), vmem((n2, dr, fd), F32), vmem((n2, fr, dm), F32),
             ),
             in_specs=[hbm] * 5,
             out_specs=(whole,) * NA,
             scratch_shapes=scratch,
-            compiler_params=pltpu.CompilerParams(collective_id=0, has_side_effects=True, vmem_limit_bytes=67043328),
+            compiler_params=pltpu.CompilerParams(collective_id=0, has_side_effects=True, vmem_limit_bytes=66300000),
             name="train_step",
         )(act_in.reshape(rows, dm), cot_out.reshape(rows, dm), w_gate[:, 0], w_in[:, 0], w_out[:, 0])
         grad_act, grad_gate, grad_lin, grad_proj = pl.pallas_call(
-            hand_on, out_shape=tuple(jax.ShapeDtypeStruct(a.shape, a.dtype) for a in out), in_specs=[hbm] * NA, out_specs=(hbm,) * NA,
-            scratch_shapes=[*(vmem(a.shape, a.dtype) for a in out), dma((NA,)), dma((NA,))], name="hand_on",
-        )(*out)
+            hand_on, out_shape=tuple(jax.ShapeDtypeStruct(a.shape, a.dtype) for a in out), in_specs=[whole] * NA, out_specs=(hbm,) * NA,
+            scratch_shapes=[dma((NA,))], compiler_params=pltpu.CompilerParams(vmem_limit_bytes=2 ** 20), name="hand_on",
+        )(*(pltpu.with_memory_space_constraint(a, vmem) for a in out))
         return grad_act.reshape(shape), grad_gate[:, None], grad_lin[:, None], grad_proj[:, None]
 
     return jax.shard_map(body, mesh=mesh, in_specs=(act_spec, act_spec, w_spec, w_spec, w_spec),

time: 117 us -> 115 us (0.983)
  Pallas kernels: 116 us -> 114 us
    pallas_call x1, Pallas kernels: 115 us -> 113 us  [body(): pl.pallas_call(kernel, out_shape=(vmem((rows, dm), BF), vmem((n2, dr, fd)...]
where the time goes in v5:
time: 115 us; the launch traced here: 114 us
  Pallas kernels  114 us (99%)
    pallas_call x1, Pallas kernels, body(): pl.pallas_call(kernel, out_shape=(vmem((rows, dm), BF), vmem((n2, dr, fd)...  113 us

profile of v5, /device:TPU:0, one launch (start us, length us, event | category | flops | bytes accessed | tf_op | source)
XLA Modules:
  0.0 114.5 jit_solution(7836008446469264676)
XLA Ops:
  0.6 112.8 %train_step.1 = (bf16[256,512]{1,0:T(8,128)(2,1)S(1)}, f32[2,8,2048]{2,1,0:T(8,128)S(1)}, f32[2,8,2048]{2,1,0:T(8,128)S(1)}, f32[2,32,512]{2,1,0:T(8,128)S(1)}) custom-call(bf16[256,512]{1,0:T(8,128)(2,1)} %bitcast.17, bf16[256,512]{1,0:T(8,128)(2,1)} %bitcast.18, bf16[2,8,2048]{2,1,0:T(8,128)(2,1)} %bitcast.19, bf16[2,8,2048]{2,1,0:T(8,128)(2,1)} %bitcast.20, ...), custom_call_target="tpu_custom_call" | custom-call | tf_op jit(solution)/shard_map/train_step/pallas_call | solution.py:662
  113.4 0.9 hand_on.1

commit v6 on v5

--- a/solution.py
+++ b/solution.py
@@ -153,6 +153,18 @@
         for half in HALVES:
             for k in (X, Y, Z):
                 small_wait(v, k, ph, OPP, half, 4 + half)
+
+    def direct_send(v):
+        for delta in (OPP, PLUS, MINUS):
+            for k in (X, Y, Z):
+                own = wts[k].at[v, zc, yc, xc]
+                send(own, own, ag_s.at[v, k, 0], ag_r.at[v, k, 0, delta], peer(AXES[k][0], delta), p)
+
+    def direct_wait(v):
+        for delta in RING:
+            for k in (X, Y, Z):
+                at = tuple(rot(coord[ax], -delta) if ax == AXES[k][0] else coord[ax] for ax in (Z, Y, X))
+                wait_recv(wts[k].at[(v,) + at], ag_r.at[v, k, 0, delta])
 
     UP, DOWN = (0, PLUS), (MINUS, OPP)
     RELAYS = ((UP[0], PLUS), (DOWN[0], MINUS), (UP[1], PLUS), (DOWN[1], MINUS))
@@ -375,9 +387,11 @@
         scatter_sum(v, which, 0)
         scatter_send(v, which, 1, MERGED + DIRECT)
 
-    def scatter_last(v):
+    def scatter_out(v):
         scatter_sum(v, OUT, 1)
         go[v] = gout[v, jb, xc]
+
+    def scatter_last(v):
         scatter_sum(v, IN, 1)
         for which in HALVES:
             fin[v, :, which] = gin[v, which, :, jb, xc]
@@ -415,9 +429,9 @@
     def pass_on(part, item, buf, which, vd):
         step(part, item[0], buf, which, vd, item[1])
 
-    ALL = UP + (MINUS, OPP), DOWN + (0, PLUS)
-    for v in BLOCKS:
-        step(small_send, v, 0)
+    AFTER = (MINUS, OPP), (0, PLUS)
+    step(direct_send, 0)
+    step(small_send, 1, 0)
 
     @on(0)
     def _():
@@ -427,11 +441,9 @@
     def _():
         step(spread_same, eb, 1, 1, mc_s.at[0])
 
-    for v in BLOCKS:
-        step(small_relay, v, 0)
-    step(small_rest, 0, 0)
-    step(small_last, 0, 0)
+    step(direct_wait, 0)
     step(small_send, 0, 1)
+    step(small_relay, 1, 0)
     step(large_send, 0, (0,), (0,))
     step(small_rest, 1, 0)
     step(small_last, 1, 0)
@@ -448,17 +460,26 @@
 
     @on(0)
     def _():
-        step(large_send, 1, *ALL)
+        step(large_send, 1, UP, DOWN)
 
     step(large_finish, 0)
 
+    @on(0)
+    def _():
+        step(large_send, 1, *AFTER)
+
     @on(1)
     def _():
         step(take_turn)
-        step(large_send, 1, *ALL)
+        step(large_send, 1, UP, DOWN)
         step(spread_own, hb, 0, 0)
 
     step(block_gates, 0)
+
+    @on(1)
+    def _():
+        step(large_send, 1, *AFTER)
+
     step(block_out, 0, h_mid[0])
     pass_on(spread_near, h_mid, hb, 0, p)
     step(large_relay, 1)
@@ -508,10 +529,6 @@
     def _():
         step(spread_relay, eb, 1, 1)
 
-    @on(1)
-    def _():
-        step(spread_relay, hb, 0, 0)
-
     step(grad_hidden, 1, EARLY)
     step(grad_out, 1, EARLY)
 
@@ -545,6 +562,7 @@
 
     @on(1)
     def _():
+        step(spread_relay, hb, 0, 0)
         step(grad_first, 0, EARLY)
 
     step(scatter_send, 1, OUT, 0, DIRECT)
@@ -557,22 +575,22 @@
 
     step(grad_hidden, 0, EARLY)
     step(scatter_send, 1, IN, 0, DIRECT)
+    step(grad_in, 0, EARLY)
+    step(scatter_relay, 1, OUT, 0)
     step(grad_out, 0, EARLY)
-    step(scatter_relay, 1, OUT, 0)
-    step(grad_in, 0, EARLY)
     step(spread_finish, eb, 1, 0)
     step(grad_hidden, 0, LATE)
-    step(grad_out, 0, LATE)
-    step(scatter_send, 0, OUT, 0, MERGED)
     step(grad_in, 0, LATE)
     step(scatter_send, 0, IN, 0, MERGED)
+    step(grad_out, 0, LATE)
     step(scatter_relay, 1, IN, 0)
+    step(scatter_send, 0, OUT, 0, MERGED)
+    step(scatter_send, 0, IN, 0, DIRECT)
+    step(scatter_turn, 1, OUT)
+    step(scatter_relay, 0, IN, 0)
     step(scatter_send, 0, OUT, 0, DIRECT)
-    step(scatter_turn, 1, OUT)
-    step(scatter_send, 0, IN, 0, DIRECT)
+    step(scatter_turn, 1, IN)
     step(scatter_relay, 0, OUT, 0)
-    step(scatter_turn, 1, IN)
-    step(scatter_relay, 0, IN, 0)
     step(scatter_relay, 1, OUT, 1)
 
     @on(1)
@@ -580,14 +598,16 @@
         wait_recv(ga, ga_r)
 
     gact[...] = ga[...]
+    step(scatter_turn, 0, IN)
+    step(scatter_relay, 1, IN, 1)
     step(scatter_turn, 0, OUT)
-    step(scatter_relay, 1, IN, 1)
-    step(scatter_turn, 0, IN)
-    step(scatter_relay, 0, OUT, 1)
+    step(scatter_out, 1)
     step(scatter_last, 1)
     step(scatter_relay, 0, IN, 1)
+    step(scatter_relay, 0, OUT, 1)
     step(scatter_last, 0)
     step(scatter_finish, 1)
+    step(scatter_out, 0)
     step(scatter_finish, 0)
 
     for v in BLOCKS:

time: 115 us -> 113 us (0.983)
  Pallas kernels: 114 us -> 112 us
    pallas_call x1, Pallas kernels: 113 us -> 111 us  [body(): pl.pallas_call(kernel, out_shape=(vmem((rows, dm), BF), vmem((n2, dr, fd)...]
where the time goes in v6:
time: 113 us
  Pallas kernels  112 us (99%)
    pallas_call x1, Pallas kernels, body(): pl.pallas_call(kernel, out_shape=(vmem((rows, dm), BF), vmem((n2, dr, fd)...  111 us

profile of v6, /device:TPU:0, one launch (start us, length us, event | category | flops | bytes accessed | tf_op | source)
XLA Modules:
  0.0 112.8 jit_solution(11165750044097454839)
XLA Ops:
  0.6 111.1 %train_step.1 = (bf16[256,512]{1,0:T(8,128)(2,1)S(1)}, f32[2,8,2048]{2,1,0:T(8,128)S(1)}, f32[2,8,2048]{2,1,0:T(8,128)S(1)}, f32[2,32,512]{2,1,0:T(8,128)S(1)}) custom-call(bf16[256,512]{1,0:T(8,128)(2,1)} %bitcast.17, bf16[256,512]{1,0:T(8,128)(2,1)} %bitcast.18, bf16[2,8,2048]{2,1,0:T(8,128)(2,1)} %bitcast.19, bf16[2,8,2048]{2,1,0:T(8,128)(2,1)} %bitcast.20, ...), custom_call_target="tpu_custom_call" | custom-call | tf_op jit(solution)/shard_map/train_step/pallas_call | solution.py:682
  111.8 0.9 hand_on.1

commit v7 on v6

--- a/solution.py
+++ b/solution.py
@@ -341,7 +341,7 @@
             cols = split(fs)[colour]
             b, x = (t, slice(None) if st == 0 else xc) if along_b else (slice(None) if st == 0 else jb, t)
             return gin.at[v, half, :, b, x, :, cols]
-        cols = pl.ds(colour * (dm // 2), dm // 2)
+        cols = split(dm)[colour]
         if st == 0:
             hs = pl.ds(2 * half, 2)
             return gout.at[v, t, hs, :, cols] if along_b else gout.at[v, hs, t, :, cols]
@@ -467,6 +467,7 @@
     @on(0)
     def _():
         step(large_send, 1, *AFTER)
+        step(give_turn)
 
     @on(1)
     def _():
@@ -486,14 +487,12 @@
 
     @on(0)
     def _():
-        step(give_turn)
         step(spread_relay, hb, 0, 0)
 
     step(large_finish, 1)
 
     @on(1)
     def _():
-        step(give_turn)
         pass_on(spread_far, h_mid, hb, 0, p)
 
     step(spread_own, hb, 0, 1)
@@ -507,9 +506,8 @@
         step(spread_finish, hb, 0, 0)
         step(grad_first, 0, EARLY)
         step(grad_first, 0, LATE)
-        step(take_turn)
+        step(spread_own, eb, 1, 1)
         pass_on(spread_far, h_mid, hb, 0, p)
-        step(spread_own, eb, 1, 1)
         step(block_backward, 1, e_first[0])
         pass_on(spread_near, e_first, eb, 1, 0)
         pass_on(spread_far, e_first, eb, 1, 0)
@@ -556,6 +554,7 @@
 
     @on(0)
     def _():
+        step(spread_relay, eb, 1, 0)
         step(spread_own, eb, 1, 0)
         step(block_backward, 0, ga)
         send(ga, ga, ga_s, ga_r, d, 1)
@@ -566,10 +565,10 @@
         step(grad_first, 0, EARLY)
 
     step(scatter_send, 1, OUT, 0, DIRECT)
-    step(spread_relay, eb, 1, 0)
-
-    @on(1)
-    def _():
+
+    @on(1)
+    def _():
+        step(spread_relay, eb, 1, 0)
         step(spread_finish, hb, 0, 0)
         step(grad_first, 0, LATE)
 
@@ -675,7 +674,7 @@
             dma((n2, n2, n2, n2)), dma((n2, n2, n2, n2, 6)), dma((n2,)), dma((n2, n3)), pltpu.SemaphoreType.REGULAR,
             *(vmem((n2, 6, *lead, width), F32)
               for lead_in, lead_out in (((*ring, dr), (n2, fr)), ((na, dr), (fr // n2,)))
-              for lead, width in ((lead_in, fs - pf), (lead_in, pf), (lead_out, dm // n2), (lead_out, dm // n2))),
+              for lead, width in ((lead_in, fs - pf), (lead_in, pf), (lead_out, dm - pf), (lead_out, pf))),
         ]
         hbm = pl.BlockSpec(memory_space=pl.ANY)
         whole = pl.BlockSpec(memory_space=pltpu.VMEM)

time: 113 us -> 116 us (1.027)
  Pallas kernels: 112 us -> 115 us
    pallas_call x1, Pallas kernels: 111 us -> 114 us  [body(): pl.pallas_call(kernel, out_shape=(vmem((rows, dm), BF), vmem((n2, dr, fd)...]
where the time goes in v7:
time: 116 us
  Pallas kernels  115 us (99%)
    pallas_call x1, Pallas kernels, body(): pl.pallas_call(kernel, out_shape=(vmem((rows, dm), BF), vmem((n2, dr, fd)...  114 us

profile of v7, /device:TPU:0, one launch (start us, length us, event | category | flops | bytes accessed | tf_op | source)
XLA Modules:
  0.0 115.6 jit_solution(6667459586067211237)
XLA Ops:
  0.6 113.9 %train_step.1 = (bf16[256,512]{1,0:T(8,128)(2,1)S(1)}, f32[2,8,2048]{2,1,0:T(8,128)S(1)}, f32[2,8,2048]{2,1,0:T(8,128)S(1)}, f32[2,32,512]{2,1,0:T(8,128)S(1)}) custom-call(bf16[256,512]{1,0:T(8,128)(2,1)} %bitcast.17, bf16[256,512]{1,0:T(8,128)(2,1)} %bitcast.18, bf16[2,8,2048]{2,1,0:T(8,128)(2,1)} %bitcast.19, bf16[2,8,2048]{2,1,0:T(8,128)(2,1)} %bitcast.20, ...), custom_call_target="tpu_custom_call" | custom-call | tf_op jit(solution)/shard_map/train_step/pallas_call | solution.py:681
  114.6 0.9 hand_on.1

commit v8 on v7

--- a/solution.py
+++ b/solution.py
@@ -19,7 +19,7 @@
 PLUS, MINUS = RING[:-1]
 QUARTERS = range(NA)
 OWN = 0
-AXES = ((X, Y, Z), (Y, Z, X), (Z, X, Y))
+AXES = ((X, Y, Z), (Y, Z, X), (Z, X, Y), (Z, Y, X))
 
 
 def mm(left, right):
@@ -116,15 +116,25 @@
 
     FIRST, REST = ((0, PLUS, 0), (1, MINUS, 2)), ((1, PLUS, 1), (0, MINUS, 3))
     LARGE = 2
+    whole = slice(None)
+
+    def parts(v):
+        return range(len(AXES) - v)
+
+    def part_at(v, k, small, middle, large, half=None):
+        place = dict(zip(AXES[k], (small, middle, large)))
+        cols = whole if v or k % 3 else (pl.ds(0, fd - fs), pl.ds(fd - fs, fs))[k // 3]
+        if half is not None:
+            width = wts[k].shape[-1] // 2
+            cols = pl.ds(half * width, width)
+        return wts[k % 3].at[v, place[Z], place[Y], place[X], :, cols]
+
+    def own(k):
+        return [coord[ax] for ax in AXES[k]]
 
     def chunk(v, k, ph, q, half):
-        if ph == 0:
-            width = wts[k].shape[-1] // 2
-            ix = tuple(q if ax == AXES[k][0] else coord[ax] for ax in (Z, Y, X)) + (slice(None), pl.ds(half * width, width))
-        else:
-            hs = pl.ds(2 * half, 2)
-            ix = ((zc, q, hs), (q, hs, xc), (hs, yc, q))[k]
-        return wts[k].at[(v,) + ix]
+        small, middle, large = own(k)
+        return part_at(v, k, q, middle, large, half) if ph == 0 else part_at(v, k, pl.ds(2 * half, 2), q, large)
 
     def small_copy(v, k, ph, q, half, delta, slot):
         ref = chunk(v, k, ph, q, half)
@@ -135,44 +145,42 @@
 
     def small_send(v, ph):
         for half, delta, slot in FIRST + REST:
-            for k in (X, Y, Z):
+            for k in parts(v):
                 small_copy(v, k, ph, coord[AXES[k][ph]], half, delta, slot)
 
     def small_relay(v, ph):
         for half, delta, slot in FIRST:
-            for k in (X, Y, Z):
+            for k in parts(v):
                 small_wait(v, k, ph, -delta, half, slot)
                 small_copy(v, k, ph, rot(coord[AXES[k][ph]], -delta), half, delta, 4 + half)
 
     def small_rest(v, ph):
         for half, delta, slot in REST:
-            for k in (X, Y, Z):
+            for k in parts(v):
                 small_wait(v, k, ph, -delta, half, slot)
 
     def small_last(v, ph):
         for half in HALVES:
-            for k in (X, Y, Z):
+            for k in parts(v):
                 small_wait(v, k, ph, OPP, half, 4 + half)
 
     def direct_send(v):
         for delta in (OPP, PLUS, MINUS):
-            for k in (X, Y, Z):
-                own = wts[k].at[v, zc, yc, xc]
-                send(own, own, ag_s.at[v, k, 0], ag_r.at[v, k, 0, delta], peer(AXES[k][0], delta), p)
+            for k in parts(v):
+                ref = part_at(v, k, *own(k))
+                send(ref, ref, ag_s.at[v, k, 0], ag_r.at[v, k, 0, delta], peer(AXES[k][0], delta), p)
 
     def direct_wait(v):
         for delta in RING:
-            for k in (X, Y, Z):
-                at = tuple(rot(coord[ax], -delta) if ax == AXES[k][0] else coord[ax] for ax in (Z, Y, X))
-                wait_recv(wts[k].at[(v,) + at], ag_r.at[v, k, 0, delta])
+            for k in parts(v):
+                small, middle, large = own(k)
+                wait_recv(part_at(v, k, rot(small, -delta), middle, large), ag_r.at[v, k, 0, delta])
 
     UP, DOWN = (0, PLUS), (MINUS, OPP)
     RELAYS = ((UP[0], PLUS), (DOWN[0], MINUS), (UP[1], PLUS), (DOWN[1], MINUS))
 
     def row(v, k, q, r):
-        m = rot(coord[AXES[k][1]], r)
-        ix = ((q, m), (m, slice(None), q), (slice(None), q, m))[k]
-        return wts[k].at[(v,) + ix]
+        return part_at(v, k, whole, rot(coord[AXES[k][1]], r), q)
 
     def large_slot(r, delta):
         return r if delta == PLUS else NA + r
@@ -180,14 +188,14 @@
     def large_send(v, up, down):
         for pair in zip(up, down):
             for r, delta in zip(pair, (PLUS, MINUS)):
-                for k in (X, Y, Z):
+                for k in parts(v):
                     ax = AXES[k][LARGE]
                     ref = row(v, k, coord[ax], r)
                     send(ref, ref, ag_s.at[v, k, LARGE], lg_r.at[v, k, large_slot(r, delta)], peer(ax, delta), p)
 
     def large_relay(v):
         for r, delta in RELAYS:
-            for k in (X, Y, Z):
+            for k in parts(v):
                 ax = AXES[k][LARGE]
                 ref = row(v, k, rot(coord[ax], -delta), r)
                 wait_recv(ref, lg_r.at[v, k, large_slot(r, delta)])
@@ -196,10 +204,10 @@
     def large_finish(v):
         for pieces, delta in ((DOWN, PLUS), (UP, MINUS)):
             for r in pieces:
-                for k in (X, Y, Z):
+                for k in parts(v):
                     wait_recv(row(v, k, rot(coord[AXES[k][LARGE]], -delta), r), lg_r.at[v, k, large_slot(r, delta)])
         for r in QUARTERS:
-            for k in (X, Y, Z):
+            for k in parts(v):
                 wait_recv(row(v, k, rot(coord[AXES[k][LARGE]], OPP), r), lg_r.at[v, k, 2 * NA + r])
 
     half_rows = rows // 2
@@ -467,7 +475,6 @@
     @on(0)
     def _():
         step(large_send, 1, *AFTER)
-        step(give_turn)
 
     @on(1)
     def _():
@@ -487,6 +494,7 @@
 
     @on(0)
     def _():
+        step(give_turn)
         step(spread_relay, hb, 0, 0)
 
     step(large_finish, 1)
@@ -539,7 +547,10 @@
     step(spread_finish, eb, 1, 1)
     step(grad_hidden, 1, LATE)
     step(grad_out, 1, LATE)
-    step(scatter_send, 1, OUT, 0, MERGED)
+
+    @on(0)
+    def _():
+        step(scatter_send, 1, OUT, 0, MERGED)
 
     @on(1)
     def _():
@@ -547,6 +558,7 @@
         step(block_backward, 0, e_last[0])
         pass_on(spread_near, e_last, eb, 1, 0)
         pass_on(spread_far, e_last, eb, 1, 0)
+        step(scatter_send, 1, OUT, 0, MERGED)
         step(grad_in, 1, EARLY)
 
     step(grad_in, 1, LATE)
@@ -610,10 +622,11 @@
     step(scatter_finish, 0)
 
     for v in BLOCKS:
-        for k in (X, Y, Z):
-            wait_send(wts[k].at[v, 0, 0, pl.ds(0, 3)], ag_s.at[v, k, 0])
-            wait_send(wts[k].at[v, 0, pl.ds(0, 3)], ag_s.at[v, k, 1])
-            wait_send(wts[k].at[v, pl.ds(0, 3)], ag_s.at[v, k, LARGE])
+        for k in parts(v):
+            three = pl.ds(0, len(RING))
+            wait_send(part_at(v, k, three, 0, 0), ag_s.at[v, k, 0])
+            wait_send(part_at(v, k, whole, three, 0), ag_s.at[v, k, 1])
+            wait_send(part_at(v, k, whole, whole, three), ag_s.at[v, k, LARGE])
         for colour in COLOURS:
             for which in HALVES:
                 for st in HALVES:
@@ -670,7 +683,7 @@
             vmem((n2, dm, fs), BF), vmem((n2, dm, fs), BF), vmem((fs, dm), BF),
             vmem((n2, n2, na, *ring, dr, fs), F32), vmem((n2, *ring, fr, dm), F32),
             vmem((n2, na, n2, dr, fs), F32), vmem((n2, n3, n2, dr, fs), F32),
-            dma((n2, na)), dma((n2, n3, n3)), dma((n2, n3, n2, 6)), dma((n2, n3, n3 * na)), dma((5,)), dma((n2, n2, 5)), dma((n2, n2)), dma, dma,
+            dma((n2, na)), dma((n2, na, n3)), dma((n2, na, n2, 6)), dma((n2, na, n3 * na)), dma((5,)), dma((n2, n2, 5)), dma((n2, n2)), dma, dma,
             dma((n2, n2, n2, n2)), dma((n2, n2, n2, n2, 6)), dma((n2,)), dma((n2, n3)), pltpu.SemaphoreType.REGULAR,
             *(vmem((n2, 6, *lead, width), F32)
               for lead_in, lead_out in (((*ring, dr), (n2, fr)), ((na, dr), (fr // n2,)))

time: 116 us -> 116 us (level)
  no operation moved by 1% of the time
where the time goes in v8:
time: 116 us
  Pallas kernels  115 us (99%)
    pallas_call x1, Pallas kernels, body(): pl.pallas_call(kernel, out_shape=(vmem((rows, dm), BF), vmem((n2, dr, fd)...  115 us

profile of v8, /device:TPU:0, one launch (start us, length us, event | category | flops | bytes accessed | tf_op | source)
XLA Modules:
  0.0 116.3 jit_solution(1970756062328938048)
XLA Ops:
  0.6 114.6 %train_step.1 = (bf16[256,512]{1,0:T(8,128)(2,1)S(1)}, f32[2,8,2048]{2,1,0:T(8,128)S(1)}, f32[2,8,2048]{2,1,0:T(8,128)S(1)}, f32[2,32,512]{2,1,0:T(8,128)S(1)}) custom-call(bf16[256,512]{1,0:T(8,128)(2,1)} %bitcast.17, bf16[256,512]{1,0:T(8,128)(2,1)} %bitcast.18, bf16[2,8,2048]{2,1,0:T(8,128)(2,1)} %bitcast.19, bf16[2,8,2048]{2,1,0:T(8,128)(2,1)} %bitcast.20, ...), custom_call_target="tpu_custom_call" | custom-call | tf_op jit(solution)/shard_map/train_step/pallas_call | solution.py:694
  115.2 0.9 hand_on.1

commit v9 on v8

--- a/solution.py
+++ b/solution.py
@@ -19,7 +19,9 @@
 PLUS, MINUS = RING[:-1]
 QUARTERS = range(NA)
 OWN = 0
-AXES = ((X, Y, Z), (Y, Z, X), (Z, X, Y), (Z, Y, X))
+AXES = ((Z, X, Y), (Y, Z, X), (X, Y, Z))
+UP_MATS, OUT_MAT = (0, 1), (2,)
+MATS = UP_MATS + OUT_MAT
 
 
 def mm(left, right):
@@ -118,16 +120,11 @@
     LARGE = 2
     whole = slice(None)
 
-    def parts(v):
-        return range(len(AXES) - v)
-
     def part_at(v, k, small, middle, large, half=None):
         place = dict(zip(AXES[k], (small, middle, large)))
-        cols = whole if v or k % 3 else (pl.ds(0, fd - fs), pl.ds(fd - fs, fs))[k // 3]
-        if half is not None:
-            width = wts[k].shape[-1] // 2
-            cols = pl.ds(half * width, width)
-        return wts[k % 3].at[v, place[Z], place[Y], place[X], :, cols]
+        width = wts[k].shape[-1] // 2
+        cols = whole if half is None else pl.ds(half * width, width)
+        return wts[k].at[v, place[Z], place[Y], place[X], :, cols]
 
     def own(k):
         return [coord[ax] for ax in AXES[k]]
@@ -145,34 +142,34 @@
 
     def small_send(v, ph):
         for half, delta, slot in FIRST + REST:
-            for k in parts(v):
+            for k in MATS:
                 small_copy(v, k, ph, coord[AXES[k][ph]], half, delta, slot)
 
     def small_relay(v, ph):
         for half, delta, slot in FIRST:
-            for k in parts(v):
+            for k in MATS:
                 small_wait(v, k, ph, -delta, half, slot)
                 small_copy(v, k, ph, rot(coord[AXES[k][ph]], -delta), half, delta, 4 + half)
 
     def small_rest(v, ph):
         for half, delta, slot in REST:
-            for k in parts(v):
+            for k in MATS:
                 small_wait(v, k, ph, -delta, half, slot)
 
     def small_last(v, ph):
         for half in HALVES:
-            for k in parts(v):
+            for k in MATS:
                 small_wait(v, k, ph, OPP, half, 4 + half)
 
     def direct_send(v):
         for delta in (OPP, PLUS, MINUS):
-            for k in parts(v):
+            for k in MATS:
                 ref = part_at(v, k, *own(k))
                 send(ref, ref, ag_s.at[v, k, 0], ag_r.at[v, k, 0, delta], peer(AXES[k][0], delta), p)
 
     def direct_wait(v):
         for delta in RING:
-            for k in parts(v):
+            for k in MATS:
                 small, middle, large = own(k)
                 wait_recv(part_at(v, k, rot(small, -delta), middle, large), ag_r.at[v, k, 0, delta])
 
@@ -188,26 +185,26 @@
     def large_send(v, up, down):
         for pair in zip(up, down):
             for r, delta in zip(pair, (PLUS, MINUS)):
-                for k in parts(v):
+                for k in MATS:
                     ax = AXES[k][LARGE]
                     ref = row(v, k, coord[ax], r)
                     send(ref, ref, ag_s.at[v, k, LARGE], lg_r.at[v, k, large_slot(r, delta)], peer(ax, delta), p)
 
     def large_relay(v):
         for r, delta in RELAYS:
-            for k in parts(v):
+            for k in MATS:
                 ax = AXES[k][LARGE]
                 ref = row(v, k, rot(coord[ax], -delta), r)
                 wait_recv(ref, lg_r.at[v, k, large_slot(r, delta)])
                 send(ref, ref, ag_s.at[v, k, LARGE], lg_r.at[v, k, 2 * NA + r], peer(ax, delta), p)
 
-    def large_finish(v):
+    def large_finish(v, mats):
         for pieces, delta in ((DOWN, PLUS), (UP, MINUS)):
             for r in pieces:
-                for k in parts(v):
+                for k in mats:
                     wait_recv(row(v, k, rot(coord[AXES[k][LARGE]], -delta), r), lg_r.at[v, k, large_slot(r, delta)])
         for r in QUARTERS:
-            for k in parts(v):
+            for k in mats:
                 wait_recv(row(v, k, rot(coord[AXES[k][LARGE]], OPP), r), lg_r.at[v, k, 2 * NA + r])
 
     half_rows = rows // 2
@@ -440,15 +437,6 @@
     AFTER = (MINUS, OPP), (0, PLUS)
     step(direct_send, 0)
     step(small_send, 1, 0)
-
-    @on(0)
-    def _():
-        step(spread_same, hb, 0, 0, mc_s.at[0])
-
-    @on(1)
-    def _():
-        step(spread_same, eb, 1, 1, mc_s.at[0])
-
     step(direct_wait, 0)
     step(small_send, 0, 1)
     step(small_relay, 1, 0)
@@ -470,7 +458,7 @@
     def _():
         step(large_send, 1, UP, DOWN)
 
-    step(large_finish, 0)
+    step(large_finish, 0, UP_MATS)
 
     @on(0)
     def _():
@@ -488,6 +476,7 @@
     def _():
         step(large_send, 1, *AFTER)
 
+    step(large_finish, 0, OUT_MAT)
     step(block_out, 0, h_mid[0])
     pass_on(spread_near, h_mid, hb, 0, p)
     step(large_relay, 1)
@@ -495,45 +484,36 @@
     @on(0)
     def _():
         step(give_turn)
-        step(spread_relay, hb, 0, 0)
-
-    step(large_finish, 1)
-
-    @on(1)
-    def _():
-        pass_on(spread_far, h_mid, hb, 0, p)
 
     step(spread_own, hb, 0, 1)
+    step(large_finish, 1, UP_MATS)
     step(block_gates, 1)
+    step(large_finish, 1, OUT_MAT)
 
     @on(0)
     def _():
         step(block_out, 1, h_late[0])
         pass_on(spread_near, h_late, hb, 0, 1)
         pass_on(spread_far, h_late, hb, 0, 1)
-        step(spread_finish, hb, 0, 0)
-        step(grad_first, 0, EARLY)
-        step(grad_first, 0, LATE)
         step(spread_own, eb, 1, 1)
         pass_on(spread_far, h_mid, hb, 0, p)
         step(block_backward, 1, e_first[0])
         pass_on(spread_near, e_first, eb, 1, 0)
         pass_on(spread_far, e_first, eb, 1, 0)
+        step(spread_same, hb, 0, 0, mc_s.at[0])
         step(spread_relay, hb, 0, 1)
 
     @on(1)
     def _():
-        step(spread_relay, hb, 0, 1)
-        step(spread_relay, eb, 1, 1)
+        pass_on(spread_far, h_mid, hb, 0, p)
+        step(spread_same, eb, 1, 1, mc_s.at[0])
         step(block_backward, 1, e_first[0])
         pass_on(spread_near, e_first, eb, 1, 1)
         pass_on(spread_far, e_first, eb, 1, 1)
+        step(spread_relay, hb, 0, 1)
 
     step(grad_first, 1, EARLY)
-
-    @on(0)
-    def _():
-        step(spread_relay, eb, 1, 1)
+    step(spread_relay, eb, 1, 1)
 
     step(grad_hidden, 1, EARLY)
     step(grad_out, 1, EARLY)
@@ -541,16 +521,7 @@
     @on(0)
     def _():
         step(grad_in, 1, EARLY)
-
-    step(spread_finish, hb, 0, 1)
-    step(grad_first, 1, LATE)
-    step(spread_finish, eb, 1, 1)
-    step(grad_hidden, 1, LATE)
-    step(grad_out, 1, LATE)
-
-    @on(0)
-    def _():
-        step(scatter_send, 1, OUT, 0, MERGED)
+        step(spread_relay, hb, 0, 0)
 
     @on(1)
     def _():
@@ -558,9 +529,19 @@
         step(block_backward, 0, e_last[0])
         pass_on(spread_near, e_last, eb, 1, 0)
         pass_on(spread_far, e_last, eb, 1, 0)
-        step(scatter_send, 1, OUT, 0, MERGED)
         step(grad_in, 1, EARLY)
 
+    step(spread_finish, hb, 0, 1)
+    step(grad_first, 1, LATE)
+
+    @on(0)
+    def _():
+        step(grad_first, 0, EARLY)
+
+    step(spread_finish, eb, 1, 1)
+    step(grad_hidden, 1, LATE)
+    step(grad_out, 1, LATE)
+    step(scatter_send, 1, OUT, 0, MERGED)
     step(grad_in, 1, LATE)
     step(scatter_send, 1, IN, 0, MERGED)
 
@@ -581,8 +562,9 @@
     @on(1)
     def _():
         step(spread_relay, eb, 1, 0)
-        step(spread_finish, hb, 0, 0)
-        step(grad_first, 0, LATE)
+
+    step(spread_finish, hb, 0, 0)
+    step(grad_first, 0, LATE)
 
     step(grad_hidden, 0, EARLY)
     step(scatter_send, 1, IN, 0, DIRECT)
@@ -622,7 +604,7 @@
     step(scatter_finish, 0)
 
     for v in BLOCKS:
-        for k in parts(v):
+        for k in MATS:
             three = pl.ds(0, len(RING))
             wait_send(part_at(v, k, three, 0, 0), ag_s.at[v, k, 0])
             wait_send(part_at(v, k, whole, three, 0), ag_s.at[v, k, 1])
@@ -683,7 +665,7 @@
             vmem((n2, dm, fs), BF), vmem((n2, dm, fs), BF), vmem((fs, dm), BF),
             vmem((n2, n2, na, *ring, dr, fs), F32), vmem((n2, *ring, fr, dm), F32),
             vmem((n2, na, n2, dr, fs), F32), vmem((n2, n3, n2, dr, fs), F32),
-            dma((n2, na)), dma((n2, na, n3)), dma((n2, na, n2, 6)), dma((n2, na, n3 * na)), dma((5,)), dma((n2, n2, 5)), dma((n2, n2)), dma, dma,
+            dma((n2, na)), dma((n2, n3, n3)), dma((n2, n3, n2, 6)), dma((n2, n3, n3 * na)), dma((5,)), dma((n2, n2, 5)), dma((n2, n2)), dma, dma,
             dma((n2, n2, n2, n2)), dma((n2, n2, n2, n2, 6)), dma((n2,)), dma((n2, n3)), pltpu.SemaphoreType.REGULAR,
             *(vmem((n2, 6, *lead, width), F32)
               for lead_in, lead_out in (((*ring, dr), (n2, fr)), ((na, dr), (fr // n2,)))

time: 116 us -> 113 us (0.974)
  Pallas kernels: 115 us -> 112 us
    pallas_call x1, Pallas kernels: 115 us -> 111 us  [body(): pl.pallas_call(kernel, out_shape=(vmem((rows, dm), BF), vmem((n2, dr, fd)...]
where the time goes in v9:
time: 113 us
  Pallas kernels  112 us (99%)
    pallas_call x1, Pallas kernels, body(): pl.pallas_call(kernel, out_shape=(vmem((rows, dm), BF), vmem((n2, dr, fd)...  111 us

profile of v9, /device:TPU:0, one launch (start us, length us, event | category | flops | bytes accessed | tf_op | source)
XLA Modules:
  0.0 112.8 jit_solution(3584133302592420602)
XLA Ops:
  0.6 111.1 %train_step.1 = (bf16[256,512]{1,0:T(8,128)(2,1)S(1)}, f32[2,8,2048]{2,1,0:T(8,128)S(1)}, f32[2,8,2048]{2,1,0:T(8,128)S(1)}, f32[2,32,512]{2,1,0:T(8,128)S(1)}) custom-call(bf16[256,512]{1,0:T(8,128)(2,1)} %bitcast.17, bf16[256,512]{1,0:T(8,128)(2,1)} %bitcast.18, bf16[2,8,2048]{2,1,0:T(8,128)(2,1)} %bitcast.19, bf16[2,8,2048]{2,1,0:T(8,128)(2,1)} %bitcast.20, ...), custom_call_target="tpu_custom_call" | custom-call | tf_op jit(solution)/shard_map/train_step/pallas_call | solution.py:676
  111.8 0.9 hand_on.1

commit v10 on v9

--- a/solution.py
+++ b/solution.py
@@ -500,7 +500,6 @@
         step(block_backward, 1, e_first[0])
         pass_on(spread_near, e_first, eb, 1, 0)
         pass_on(spread_far, e_first, eb, 1, 0)
-        step(spread_same, hb, 0, 0, mc_s.at[0])
         step(spread_relay, hb, 0, 1)
 
     @on(1)
@@ -521,7 +520,7 @@
     @on(0)
     def _():
         step(grad_in, 1, EARLY)
-        step(spread_relay, hb, 0, 0)
+        step(spread_same, hb, 0, 0, mc_s.at[0])
 
     @on(1)
     def _():
@@ -533,10 +532,6 @@
 
     step(spread_finish, hb, 0, 1)
     step(grad_first, 1, LATE)
-
-    @on(0)
-    def _():
-        step(grad_first, 0, EARLY)
 
     step(spread_finish, eb, 1, 1)
     step(grad_hidden, 1, LATE)
@@ -552,25 +547,21 @@
         step(block_backward, 0, ga)
         send(ga, ga, ga_s, ga_r, d, 1)
 
+    step(spread_relay, hb, 0, 0)
+    step(scatter_send, 1, OUT, 0, DIRECT)
+    step(grad_first, 0, EARLY)
+
     @on(1)
     def _():
-        step(spread_relay, hb, 0, 0)
-        step(grad_first, 0, EARLY)
-
-    step(scatter_send, 1, OUT, 0, DIRECT)
-
-    @on(1)
-    def _():
         step(spread_relay, eb, 1, 0)
-
-    step(spread_finish, hb, 0, 0)
-    step(grad_first, 0, LATE)
 
     step(grad_hidden, 0, EARLY)
     step(scatter_send, 1, IN, 0, DIRECT)
     step(grad_in, 0, EARLY)
+    step(grad_out, 0, EARLY)
+    step(spread_finish, hb, 0, 0)
+    step(grad_first, 0, LATE)
     step(scatter_relay, 1, OUT, 0)
-    step(grad_out, 0, EARLY)
     step(spread_finish, eb, 1, 0)
     step(grad_hidden, 0, LATE)
     step(grad_in, 0, LATE)

time: 113 us -> 115 us (1.018)
  Pallas kernels: 112 us -> 114 us
    pallas_call x1, Pallas kernels: 111 us -> 114 us  [body(): pl.pallas_call(kernel, out_shape=(vmem((rows, dm), BF), vmem((n2, dr, fd)...]
where the time goes in v10:
time: 115 us
  Pallas kernels  114 us (99%)
    pallas_call x1, Pallas kernels, body(): pl.pallas_call(kernel, out_shape=(vmem((rows, dm), BF), vmem((n2, dr, fd)...  114 us

profile of v10, /device:TPU:0, one launch (start us, length us, event | category | flops | bytes accessed | tf_op | source)
XLA Modules:
  0.0 115.2 jit_solution(12036764757337609495)
XLA Ops:
  0.6 113.5 %train_step.1 = (bf16[256,512]{1,0:T(8,128)(2,1)S(1)}, f32[2,8,2048]{2,1,0:T(8,128)S(1)}, f32[2,8,2048]{2,1,0:T(8,128)S(1)}, f32[2,32,512]{2,1,0:T(8,128)S(1)}) custom-call(bf16[256,512]{1,0:T(8,128)(2,1)} %bitcast.17, bf16[256,512]{1,0:T(8,128)(2,1)} %bitcast.18, bf16[2,8,2048]{2,1,0:T(8,128)(2,1)} %bitcast.19, bf16[2,8,2048]{2,1,0:T(8,128)(2,1)} %bitcast.20, ...), custom_call_target="tpu_custom_call" | custom-call | tf_op jit(solution)/shard_map/train_step/pallas_call | solution.py:667
  114.2 0.9 hand_on.1

commit v11 on v10

--- a/solution.py
+++ b/solution.py
@@ -42,7 +42,7 @@
 
 def kernel(act, cot, wg_in, wi_in, wo_in, gact, gg, gi, go,
            wg, wi, wo, hb, eb, xo, ga, ng, f1, f2, f1s, f2s, us, ub, da, db, das, dbs, qs, gs, is_, os_,
-           gin, gout, fin, r3,
+           gin0, gin1, gout0, gout1, fin, r3,
            lsem, ag_s, ag_r, lg_r, mc_s, mc_r, rl_s, ga_s, ga_r, rs_s, rs_r, r3_s, r3_r, turn, *rg):
     dm, fd = wo.shape[-1], wg.shape[-1]
     dr, fr = dm // NL, fd // NL
@@ -50,6 +50,7 @@
     pf = fs // NA
     rows = act.shape[0]
     wts = (wg, wi, wo)
+    gin, gout = (gin0, gin1), (gout0, gout1)
 
     p = lax.axis_index("stage")
     d = lax.axis_index("data")
@@ -315,43 +316,46 @@
             das[s] = (t * f1s[v, s]).astype(BF)
             dbs[s] = (t * f2s[v, s]).astype(BF)
 
+    def split(width):
+        return pl.ds(0, width - pf), pl.ds(width - pf, pf)
+
+    def keep(refs, v, place, tile, cols, first):
+        b, rest = place[0], place[1:]
+        lead = () if v is None else (v,)
+        for colour in COLOURS:
+            part = tile[..., cols[colour].start:cols[colour].start + cols[colour].size]
+            at = lead + ((b, slice(None)) if colour == 0 else (slice(None), b)) + rest
+            refs[colour][at] = part if first else refs[colour][at] + part
+
     def rows_of(slots):
         return pl.ds(slots[0], len(slots)), len(slots) * rows
 
     def grad_out(v, slots):
         some, count = rows_of(slots)
         for i in HALVES:
-            cols, to = pl.ds(i * 2 * pf, 2 * pf), pl.ds(2 * i, 2)
-            g = mm_tn(us[v, some, :, cols].reshape(count, 2 * pf), eb[v, some].reshape(count, dm)).reshape(2, 4, fr, dm)
-            gout[v, to] = g if OWN in slots else gout[v, to] + g
+            cols = pl.ds(i * 2 * pf, 2 * pf)
+            g = mm_tn(us[v, some, :, cols].reshape(count, 2 * pf), eb[v, some].reshape(count, dm)).reshape(2, NA, fr, dm)
+            for b in HALVES:
+                keep(gout, v, (2 * i + b,), g[b], split(dm), OWN in slots)
 
     def grad_in(v, slots):
         some, count = rows_of(slots)
         for which, dref in enumerate((das, dbs)):
             for i in QUARTERS:
                 cols = pl.ds(i * (dm // NA), dm // NA)
-                g = mm_tn(ng[v, some, :, cols].reshape(count, dm // NA), dref[some].reshape(count, fs)).reshape(4, 4, dr, fs)
+                g = mm_tn(ng[v, some, :, cols].reshape(count, dm // NA), dref[some].reshape(count, fs)).reshape(NA, NA, dr, fs)
                 for y in QUARTERS:
-                    at = (v, which, y + p * (i - y), i + p * (y - i))
-                    gin[at] = g[y] if OWN in slots else gin[at] + g[y]
+                    keep([ref.at[v, which] for ref in gin], None, (i + p * (y - i), y + p * (i - y)), g[y], split(fs), OWN in slots)
 
     IN, OUT = 0, 1
 
-    def split(width):
-        return pl.ds(0, width - pf), pl.ds(width - pf, pf)
-
     def view(which, st, v, colour, t, half):
-        along_b = colour == st
+        own = jb if colour == 0 else xc
         if which == IN:
-            cols = split(fs)[colour]
-            b, x = (t, slice(None) if st == 0 else xc) if along_b else (slice(None) if st == 0 else jb, t)
-            return gin.at[v, half, :, b, x, :, cols]
-        cols = split(dm)[colour]
-        if st == 0:
-            hs = pl.ds(2 * half, 2)
-            return gout.at[v, t, hs, :, cols] if along_b else gout.at[v, hs, t, :, cols]
-        hs = pl.ds(half * (fr // 2), fr // 2)
-        return gout.at[v, t, xc, hs, cols] if along_b else gout.at[v, jb, t, hs, cols]
+            ref = gin[colour].at[v, half]
+            return ref.at[t] if st == 0 else ref.at[own, t]
+        ref = gout[colour].at[v]
+        return ref.at[t, pl.ds(2 * half, 2)] if st == 0 else ref.at[own, t, pl.ds(half * (fr // 2), fr // 2)]
 
     RECV = (((rg[0], rg[1]), (rg[2], rg[3])), ((rg[4], rg[5]), (rg[6], rg[7])))
     MERGED, DIRECT = ((0, OPP, PLUS, 0), (1, OPP, MINUS, 1)), ((1, PLUS, PLUS, 2), (0, MINUS, MINUS, 3))
@@ -394,12 +398,14 @@
 
     def scatter_out(v):
         scatter_sum(v, OUT, 1)
-        go[v] = gout[v, jb, xc]
+        for colour in COLOURS:
+            go[v, :, split(dm)[colour]] = gout[colour][(v, jb, xc) if colour == 0 else (v, xc, jb)]
 
     def scatter_last(v):
         scatter_sum(v, IN, 1)
         for which in HALVES:
-            fin[v, :, which] = gin[v, which, :, jb, xc]
+            for colour in COLOURS:
+                fin[v, :, which, :, split(fs)[colour]] = gin[colour][(v, which, jb, xc) if colour == 0 else (v, which, xc, jb)]
         for delta in (OPP, PLUS, MINUS):
             send(fin.at[v, rot(ja, delta)], r3.at[v, delta - 1], r3_s.at[v], r3_r.at[v, delta - 1], peer_a(delta), p)
 
@@ -437,6 +443,11 @@
     AFTER = (MINUS, OPP), (0, PLUS)
     step(direct_send, 0)
     step(small_send, 1, 0)
+
+    @on(0)
+    def _():
+        step(spread_same, hb, 0, 0, mc_s.at[0])
+
     step(direct_wait, 0)
     step(small_send, 0, 1)
     step(small_relay, 1, 0)
@@ -484,6 +495,7 @@
     @on(0)
     def _():
         step(give_turn)
+        step(spread_relay, hb, 0, 0)
 
     step(spread_own, hb, 0, 1)
     step(large_finish, 1, UP_MATS)
@@ -495,6 +507,9 @@
         step(block_out, 1, h_late[0])
         pass_on(spread_near, h_late, hb, 0, 1)
         pass_on(spread_far, h_late, hb, 0, 1)
+        step(spread_finish, hb, 0, 0)
+        step(grad_first, 0, EARLY)
+        step(grad_first, 0, LATE)
         step(spread_own, eb, 1, 1)
         pass_on(spread_far, h_mid, hb, 0, p)
         step(block_backward, 1, e_first[0])
@@ -520,7 +535,6 @@
     @on(0)
     def _():
         step(grad_in, 1, EARLY)
-        step(spread_same, hb, 0, 0, mc_s.at[0])
 
     @on(1)
     def _():
@@ -547,20 +561,23 @@
         step(block_backward, 0, ga)
         send(ga, ga, ga_s, ga_r, d, 1)
 
-    step(spread_relay, hb, 0, 0)
+    @on(1)
+    def _():
+        step(spread_relay, hb, 0, 0)
+        step(grad_first, 0, EARLY)
+
     step(scatter_send, 1, OUT, 0, DIRECT)
-    step(grad_first, 0, EARLY)
 
     @on(1)
     def _():
         step(spread_relay, eb, 1, 0)
+        step(spread_finish, hb, 0, 0)
+        step(grad_first, 0, LATE)
 
     step(grad_hidden, 0, EARLY)
     step(scatter_send, 1, IN, 0, DIRECT)
     step(grad_in, 0, EARLY)
     step(grad_out, 0, EARLY)
-    step(spread_finish, hb, 0, 0)
-    step(grad_first, 0, LATE)
     step(scatter_relay, 1, OUT, 0)
     step(spread_finish, eb, 1, 0)
     step(grad_hidden, 0, LATE)
@@ -654,7 +671,8 @@
             vmem((na, rows, fs), BF), vmem((na, rows, fs), BF),
             vmem((rows, dm), F32),
             vmem((n2, dm, fs), BF), vmem((n2, dm, fs), BF), vmem((fs, dm), BF),
-            vmem((n2, n2, na, *ring, dr, fs), F32), vmem((n2, *ring, fr, dm), F32),
+            *(vmem((n2, n2, *ring, na, dr, width), F32) for width in (fs - pf, pf)),
+            *(vmem((n2, *ring, fr, width), F32) for width in (dm - pf, pf)),
             vmem((n2, na, n2, dr, fs), F32), vmem((n2, n3, n2, dr, fs), F32),
             dma((n2, na)), dma((n2, n3, n3)), dma((n2, n3, n2, 6)), dma((n2, n3, n3 * na)), dma((5,)), dma((n2, n2, 5)), dma((n2, n2)), dma, dma,
             dma((n2, n2, n2, n2)), dma((n2, n2, n2, n2, 6)), dma((n2,)), dma((n2, n3)), pltpu.SemaphoreType.REGULAR,

time: 115 us -> 113 us (0.983)
  Pallas kernels: 114 us -> 112 us
    pallas_call x1, Pallas kernels: 114 us -> 111 us  [body(): pl.pallas_call(kernel, out_shape=(vmem((rows, dm), BF), vmem((n2, dr, fd)...]
where the time goes in v11:
time: 113 us
  Pallas kernels  112 us (99%)
    pallas_call x1, Pallas kernels, body(): pl.pallas_call(kernel, out_shape=(vmem((rows, dm), BF), vmem((n2, dr, fd)...  111 us

profile of v11, /device:TPU:0, one launch (start us, length us, event | category | flops | bytes accessed | tf_op | source)
XLA Modules:
  0.0 112.7 jit_solution(17497706891080650098)
XLA Ops:
  0.6 111.0 %train_step.1 = (bf16[256,512]{1,0:T(8,128)(2,1)S(1)}, f32[2,8,2048]{2,1,0:T(8,128)S(1)}, f32[2,8,2048]{2,1,0:T(8,128)S(1)}, f32[2,32,512]{2,1,0:T(8,128)S(1)}) custom-call(bf16[256,512]{1,0:T(8,128)(2,1)} %bitcast.17, bf16[256,512]{1,0:T(8,128)(2,1)} %bitcast.18, bf16[2,8,2048]{2,1,0:T(8,128)(2,1)} %bitcast.19, bf16[2,8,2048]{2,1,0:T(8,128)(2,1)} %bitcast.20, ...), custom_call_target="tpu_custom_call" | custom-call | tf_op jit(solution)/shard_map/train_step/pallas_call | solution.py:685
  111.6 0.9 hand_on.1

commit v12 on v11

--- a/solution.py
+++ b/solution.py
@@ -214,23 +214,30 @@
     def spread_near(src, buf, which, vd, ssem):
         send(src, buf.at[vd, OWN], ssem, mc_r.at[which, vd, OWN], d, 1 - p)
 
+    def rows_half(half):
+        return pl.ds(half * half_rows, half_rows)
+
+    HALF_ORDER = [(half if first else 1 - half, slot, delta, slot if first else FAR + 1 + slot)
+                  for first in (True, False) for half, slot, delta in ((0, BACK, PLUS), (1, AHEAD, MINUS))]
+
     def spread_far(src, buf, which, vd, ssem):
-        send(src, buf.at[vd, BACK], ssem, mc_r.at[which, vd, BACK], peer_b(PLUS), 1 - p)
-        send(src, buf.at[vd, AHEAD], ssem, mc_r.at[which, vd, AHEAD], peer_b(MINUS), 1 - p)
+        for half, slot, delta, sem in HALF_ORDER:
+            send(src.at[rows_half(half)], buf.at[vd, slot, rows_half(half)], ssem, mc_r.at[which, vd, sem], peer_b(delta), 1 - p)
 
     def spread_same(buf, which, v, ssem):
-        send(buf.at[v, OWN], buf.at[v, BACK], ssem, mc_r.at[which, v, BACK], peer_a(PLUS), p)
-        send(buf.at[v, OWN], buf.at[v, AHEAD], ssem, mc_r.at[which, v, AHEAD], peer_a(MINUS), p)
+        for half, slot, delta, sem in HALF_ORDER:
+            send(buf.at[v, OWN, rows_half(half)], buf.at[v, slot, rows_half(half)], ssem, mc_r.at[which, v, sem], peer_a(delta), p)
 
     def spread_relay(buf, which, v):
-        for half, slot, delta in ((0, BACK, PLUS), (1, AHEAD, MINUS)):
-            wait_recv(buf.at[v, slot], mc_r.at[which, v, slot])
-            part = pl.ds(half * half_rows, half_rows)
-            send(buf.at[v, slot, part], buf.at[v, FAR, part], rl_s.at[which, v], mc_r.at[which, v, FAR + half], peer_a(delta), p)
+        for half, slot, delta, sem in HALF_ORDER:
+            ref = buf.at[v, slot, rows_half(half)]
+            wait_recv(ref, mc_r.at[which, v, sem])
+            if sem == slot:
+                send(ref, buf.at[v, FAR, rows_half(half)], rl_s.at[which, v], mc_r.at[which, v, FAR + half], peer_a(delta), p)
 
     def spread_finish(buf, which, v):
         for half in HALVES:
-            wait_recv(buf.at[v, FAR, pl.ds(half * half_rows, half_rows)], mc_r.at[which, v, FAR + half])
+            wait_recv(buf.at[v, FAR, rows_half(half)], mc_r.at[which, v, FAR + half])
 
     def spread_own(buf, which, v):
         wait_recv(buf.at[v, OWN], mc_r.at[which, v, OWN])
@@ -602,9 +609,9 @@
     step(scatter_turn, 0, IN)
     step(scatter_relay, 1, IN, 1)
     step(scatter_turn, 0, OUT)
+    step(scatter_relay, 0, IN, 1)
     step(scatter_out, 1)
     step(scatter_last, 1)
-    step(scatter_relay, 0, IN, 1)
     step(scatter_relay, 0, OUT, 1)
     step(scatter_last, 0)
     step(scatter_finish, 1)
@@ -674,7 +681,7 @@
             *(vmem((n2, n2, *ring, na, dr, width), F32) for width in (fs - pf, pf)),
             *(vmem((n2, *ring, fr, width), F32) for width in (dm - pf, pf)),
             vmem((n2, na, n2, dr, fs), F32), vmem((n2, n3, n2, dr, fs), F32),
-            dma((n2, na)), dma((n2, n3, n3)), dma((n2, n3, n2, 6)), dma((n2, n3, n3 * na)), dma((5,)), dma((n2, n2, 5)), dma((n2, n2)), dma, dma,
+            dma((n2, na)), dma((n2, n3, n3)), dma((n2, n3, n2, 6)), dma((n2, n3, n3 * na)), dma((5,)), dma((n2, n2, 7)), dma((n2, n2)), dma, dma,
             dma((n2, n2, n2, n2)), dma((n2, n2, n2, n2, 6)), dma((n2,)), dma((n2, n3)), pltpu.SemaphoreType.REGULAR,
             *(vmem((n2, 6, *lead, width), F32)
               for lead_in, lead_out in (((*ring, dr), (n2, fr)), ((na, dr), (fr // n2,)))

time: 113 us -> 110 us (0.973)
  Pallas kernels: 112 us -> 109 us
    pallas_call x1, Pallas kernels: 111 us -> 109 us  [body(): pl.pallas_call(kernel, out_shape=(vmem((rows, dm), BF), vmem((n2, dr, fd)...]
where the time goes in v12:
time: 110 us
  Pallas kernels  109 us (99%)
    pallas_call x1, Pallas kernels, body(): pl.pallas_call(kernel, out_shape=(vmem((rows, dm), BF), vmem((n2, dr, fd)...  109 us

profile of v12, /device:TPU:0, one launch (start us, length us, event | category | flops | bytes accessed | tf_op | source)
XLA Modules:
  0.0 110.2 jit_solution(13042756429314487294)
XLA Ops:
  0.6 108.5 %train_step.1 = (bf16[256,512]{1,0:T(8,128)(2,1)S(1)}, f32[2,8,2048]{2,1,0:T(8,128)S(1)}, f32[2,8,2048]{2,1,0:T(8,128)S(1)}, f32[2,32,512]{2,1,0:T(8,128)S(1)}) custom-call(bf16[256,512]{1,0:T(8,128)(2,1)} %bitcast.17, bf16[256,512]{1,0:T(8,128)(2,1)} %bitcast.18, bf16[2,8,2048]{2,1,0:T(8,128)(2,1)} %bitcast.19, bf16[2,8,2048]{2,1,0:T(8,128)(2,1)} %bitcast.20, ...), custom_call_target="tpu_custom_call" | custom-call | tf_op jit(solution)/shard_map/train_step/pallas_call | solution.py:692
  109.2 0.9 hand_on.1

commit v13 on v12

--- a/solution.py
+++ b/solution.py
@@ -371,25 +371,25 @@
     def axis_of(colour, st):
         return (jb, peer_b) if colour == st else (xc, functools.partial(peer, X))
 
-    def scatter_send(v, which, st, copies):
-        for colour in COLOURS:
+    def scatter_send(v, which, st, copies, colours):
+        for colour in colours:
             q, to = axis_of(colour, st)
             for half, c, delta, slot in copies:
                 send(view(which, st, v, colour, rot(q, c), half), RECV[st][which][colour].at[v, slot],
                      rs_s.at[st, v, colour, which], rs_r.at[st, v, colour, which, slot], to(delta), p)
 
-    def scatter_relay(v, which, st):
-        for colour in COLOURS:
+    def scatter_relay(v, which, st, colours):
+        for colour in colours:
             q, _ = axis_of(colour, st)
             recv = RECV[st][which][colour]
             for half, c, _, slot in RELAYED:
                 wait_recv(recv.at[v, slot - 4], rs_r.at[st, v, colour, which, slot - 4])
                 ref = view(which, st, v, colour, rot(q, c), half)
                 ref[...] = ref[...] + recv[v, slot - 4]
-        scatter_send(v, which, st, RELAYED)
-
-    def scatter_sum(v, which, st):
-        for colour in COLOURS:
+        scatter_send(v, which, st, RELAYED, colours)
+
+    def scatter_sum(v, which, st, colours):
+        for colour in colours:
             q, _ = axis_of(colour, st)
             recv = RECV[st][which][colour]
             for half in HALVES:
@@ -399,17 +399,17 @@
                 ref = view(which, st, v, colour, q, half)
                 ref[...] = ref[...] + recv[v, direct] + recv[v, merged]
 
-    def scatter_turn(v, which):
-        scatter_sum(v, which, 0)
-        scatter_send(v, which, 1, MERGED + DIRECT)
+    def scatter_turn(v, which, colours):
+        scatter_sum(v, which, 0, colours)
+        scatter_send(v, which, 1, MERGED + DIRECT, colours)
 
     def scatter_out(v):
-        scatter_sum(v, OUT, 1)
+        scatter_sum(v, OUT, 1, COLOURS)
         for colour in COLOURS:
             go[v, :, split(dm)[colour]] = gout[colour][(v, jb, xc) if colour == 0 else (v, xc, jb)]
 
     def scatter_last(v):
-        scatter_sum(v, IN, 1)
+        scatter_sum(v, IN, 1, COLOURS)
         for which in HALVES:
             for colour in COLOURS:
                 fin[v, :, which, :, split(fs)[colour]] = gin[colour][(v, which, jb, xc) if colour == 0 else (v, which, xc, jb)]
@@ -557,9 +557,15 @@
     step(spread_finish, eb, 1, 1)
     step(grad_hidden, 1, LATE)
     step(grad_out, 1, LATE)
-    step(scatter_send, 1, OUT, 0, MERGED)
+    B_FIRST, X_FIRST = (0,), (1,)
+
+    def scatter_start(v, which):
+        scatter_send(v, which, 0, MERGED + DIRECT, X_FIRST)
+        scatter_send(v, which, 0, MERGED, B_FIRST)
+
+    step(scatter_start, 1, OUT)
     step(grad_in, 1, LATE)
-    step(scatter_send, 1, IN, 0, MERGED)
+    step(scatter_start, 1, IN)
 
     @on(0)
     def _():
@@ -573,7 +579,8 @@
         step(spread_relay, hb, 0, 0)
         step(grad_first, 0, EARLY)
 
-    step(scatter_send, 1, OUT, 0, DIRECT)
+    step(scatter_send, 1, OUT, 0, DIRECT, B_FIRST)
+    step(scatter_relay, 1, OUT, 0, X_FIRST)
 
     @on(1)
     def _():
@@ -581,40 +588,48 @@
         step(spread_finish, hb, 0, 0)
         step(grad_first, 0, LATE)
 
+    step(scatter_relay, 1, IN, 0, X_FIRST)
     step(grad_hidden, 0, EARLY)
-    step(scatter_send, 1, IN, 0, DIRECT)
+    step(scatter_send, 1, IN, 0, DIRECT, B_FIRST)
     step(grad_in, 0, EARLY)
+    step(scatter_turn, 1, OUT, X_FIRST)
     step(grad_out, 0, EARLY)
-    step(scatter_relay, 1, OUT, 0)
+    step(scatter_turn, 1, IN, X_FIRST)
+    step(scatter_relay, 1, OUT, 0, B_FIRST)
     step(spread_finish, eb, 1, 0)
     step(grad_hidden, 0, LATE)
     step(grad_in, 0, LATE)
-    step(scatter_send, 0, IN, 0, MERGED)
+    step(scatter_start, 0, IN)
     step(grad_out, 0, LATE)
-    step(scatter_relay, 1, IN, 0)
-    step(scatter_send, 0, OUT, 0, MERGED)
-    step(scatter_send, 0, IN, 0, DIRECT)
-    step(scatter_turn, 1, OUT)
-    step(scatter_relay, 0, IN, 0)
-    step(scatter_send, 0, OUT, 0, DIRECT)
-    step(scatter_turn, 1, IN)
-    step(scatter_relay, 0, OUT, 0)
-    step(scatter_relay, 1, OUT, 1)
+    step(scatter_relay, 1, IN, 0, B_FIRST)
+    step(scatter_start, 0, OUT)
+    step(scatter_send, 0, IN, 0, DIRECT, B_FIRST)
+    step(scatter_turn, 1, OUT, B_FIRST)
+    step(scatter_relay, 0, IN, 0, X_FIRST)
+    step(scatter_relay, 0, OUT, 0, X_FIRST)
+    step(scatter_relay, 0, IN, 0, B_FIRST)
+    step(scatter_send, 0, OUT, 0, DIRECT, B_FIRST)
+    step(scatter_turn, 0, IN, X_FIRST)
+    step(scatter_turn, 0, OUT, X_FIRST)
+    step(scatter_turn, 1, IN, B_FIRST)
+    step(scatter_relay, 1, OUT, 1, COLOURS)
+    step(scatter_relay, 0, OUT, 0, B_FIRST)
 
     @on(1)
     def _():
         wait_recv(ga, ga_r)
 
     gact[...] = ga[...]
-    step(scatter_turn, 0, IN)
-    step(scatter_relay, 1, IN, 1)
-    step(scatter_turn, 0, OUT)
-    step(scatter_relay, 0, IN, 1)
+    step(scatter_relay, 1, IN, 1, COLOURS)
     step(scatter_out, 1)
+    step(scatter_turn, 0, IN, B_FIRST)
+    step(scatter_relay, 0, IN, 1, X_FIRST)
+    step(scatter_turn, 0, OUT, B_FIRST)
     step(scatter_last, 1)
-    step(scatter_relay, 0, OUT, 1)
+    step(scatter_relay, 0, IN, 1, B_FIRST)
+    step(scatter_relay, 0, OUT, 1, COLOURS)
+    step(scatter_finish, 1)
     step(scatter_last, 0)
-    step(scatter_finish, 1)
     step(scatter_out, 0)
     step(scatter_finish, 0)
 

time: 110 us -> 114 us (1.036)
  Pallas kernels: 109 us -> 113 us
    pallas_call x1, Pallas kernels: 109 us -> 112 us  [body(): pl.pallas_call(kernel, out_shape=(vmem((rows, dm), BF), vmem((n2, dr, fd)...]
where the time goes in v13:
time: 114 us
  Pallas kernels  113 us (99%)
    pallas_call x1, Pallas kernels, body(): pl.pallas_call(kernel, out_shape=(vmem((rows, dm), BF), vmem((n2, dr, fd)...  112 us

profile of v13, /device:TPU:0, one launch (start us, length us, event | category | flops | bytes accessed | tf_op | source)
XLA Modules:
  0.0 113.7 jit_solution(16810613651341219937)
XLA Ops:
  0.6 112.0 %train_step.1 = (bf16[256,512]{1,0:T(8,128)(2,1)S(1)}, f32[2,8,2048]{2,1,0:T(8,128)S(1)}, f32[2,8,2048]{2,1,0:T(8,128)S(1)}, f32[2,32,512]{2,1,0:T(8,128)S(1)}) custom-call(bf16[256,512]{1,0:T(8,128)(2,1)} %bitcast.17, bf16[256,512]{1,0:T(8,128)(2,1)} %bitcast.18, bf16[2,8,2048]{2,1,0:T(8,128)(2,1)} %bitcast.19, bf16[2,8,2048]{2,1,0:T(8,128)(2,1)} %bitcast.20, ...), custom_call_target="tpu_custom_call" | custom-call | tf_op jit(solution)/shard_map/train_step/pallas_call | solution.py:707
  112.6 0.9 hand_on.1

commit v14 on v12

--- a/solution.py
+++ b/solution.py
@@ -323,8 +323,10 @@
             das[s] = (t * f1s[v, s]).astype(BF)
             dbs[s] = (t * f2s[v, s]).astype(BF)
 
-    def split(width):
-        return pl.ds(0, width - pf), pl.ds(width - pf, pf)
+    def split(width, second):
+        return pl.ds(0, width - second), pl.ds(width - second, second)
+
+    IN_COLS, OUT_COLS = split(fs, pf), split(dm, dm // 2)
 
     def keep(refs, v, place, tile, cols, first):
         b, rest = place[0], place[1:]
@@ -343,7 +345,7 @@
             cols = pl.ds(i * 2 * pf, 2 * pf)
             g = mm_tn(us[v, some, :, cols].reshape(count, 2 * pf), eb[v, some].reshape(count, dm)).reshape(2, NA, fr, dm)
             for b in HALVES:
-                keep(gout, v, (2 * i + b,), g[b], split(dm), OWN in slots)
+                keep(gout, v, (2 * i + b,), g[b], OUT_COLS, OWN in slots)
 
     def grad_in(v, slots):
         some, count = rows_of(slots)
@@ -352,7 +354,7 @@
                 cols = pl.ds(i * (dm // NA), dm // NA)
                 g = mm_tn(ng[v, some, :, cols].reshape(count, dm // NA), dref[some].reshape(count, fs)).reshape(NA, NA, dr, fs)
                 for y in QUARTERS:
-                    keep([ref.at[v, which] for ref in gin], None, (i + p * (y - i), y + p * (i - y)), g[y], split(fs), OWN in slots)
+                    keep([ref.at[v, which] for ref in gin], None, (i + p * (y - i), y + p * (i - y)), g[y], IN_COLS, OWN in slots)
 
     IN, OUT = 0, 1
 
@@ -406,13 +408,13 @@
     def scatter_out(v):
         scatter_sum(v, OUT, 1)
         for colour in COLOURS:
-            go[v, :, split(dm)[colour]] = gout[colour][(v, jb, xc) if colour == 0 else (v, xc, jb)]
+            go[v, :, OUT_COLS[colour]] = gout[colour][(v, jb, xc) if colour == 0 else (v, xc, jb)]
 
     def scatter_last(v):
         scatter_sum(v, IN, 1)
         for which in HALVES:
             for colour in COLOURS:
-                fin[v, :, which, :, split(fs)[colour]] = gin[colour][(v, which, jb, xc) if colour == 0 else (v, which, xc, jb)]
+                fin[v, :, which, :, IN_COLS[colour]] = gin[colour][(v, which, jb, xc) if colour == 0 else (v, which, xc, jb)]
         for delta in (OPP, PLUS, MINUS):
             send(fin.at[v, rot(ja, delta)], r3.at[v, delta - 1], r3_s.at[v], r3_r.at[v, delta - 1], peer_a(delta), p)
 
@@ -549,6 +551,7 @@
         step(block_backward, 0, e_last[0])
         pass_on(spread_near, e_last, eb, 1, 0)
         pass_on(spread_far, e_last, eb, 1, 0)
+        step(spread_relay, hb, 0, 0)
         step(grad_in, 1, EARLY)
 
     step(spread_finish, hb, 0, 1)
@@ -560,29 +563,22 @@
     step(scatter_send, 1, OUT, 0, MERGED)
     step(grad_in, 1, LATE)
     step(scatter_send, 1, IN, 0, MERGED)
+    step(scatter_send, 1, OUT, 0, DIRECT)
+    step(scatter_send, 1, IN, 0, DIRECT)
 
     @on(0)
     def _():
         step(spread_relay, eb, 1, 0)
         step(spread_own, eb, 1, 0)
-        step(block_backward, 0, ga)
-        send(ga, ga, ga_s, ga_r, d, 1)
 
     @on(1)
     def _():
-        step(spread_relay, hb, 0, 0)
         step(grad_first, 0, EARLY)
-
-    step(scatter_send, 1, OUT, 0, DIRECT)
-
-    @on(1)
-    def _():
         step(spread_relay, eb, 1, 0)
         step(spread_finish, hb, 0, 0)
         step(grad_first, 0, LATE)
 
     step(grad_hidden, 0, EARLY)
-    step(scatter_send, 1, IN, 0, DIRECT)
     step(grad_in, 0, EARLY)
     step(grad_out, 0, EARLY)
     step(scatter_relay, 1, OUT, 0)
@@ -594,6 +590,12 @@
     step(scatter_relay, 1, IN, 0)
     step(scatter_send, 0, OUT, 0, MERGED)
     step(scatter_send, 0, IN, 0, DIRECT)
+
+    @on(0)
+    def _():
+        step(block_backward, 0, ga)
+        send(ga, ga, ga_s, ga_r, d, 1)
+
     step(scatter_turn, 1, OUT)
     step(scatter_relay, 0, IN, 0)
     step(scatter_send, 0, OUT, 0, DIRECT)
@@ -679,13 +681,13 @@
             vmem((rows, dm), F32),
             vmem((n2, dm, fs), BF), vmem((n2, dm, fs), BF), vmem((fs, dm), BF),
             *(vmem((n2, n2, *ring, na, dr, width), F32) for width in (fs - pf, pf)),
-            *(vmem((n2, *ring, fr, width), F32) for width in (dm - pf, pf)),
+            *(vmem((n2, *ring, fr, width), F32) for width in (dm // n2, dm // n2)),
             vmem((n2, na, n2, dr, fs), F32), vmem((n2, n3, n2, dr, fs), F32),
             dma((n2, na)), dma((n2, n3, n3)), dma((n2, n3, n2, 6)), dma((n2, n3, n3 * na)), dma((5,)), dma((n2, n2, 7)), dma((n2, n2)), dma, dma,
             dma((n2, n2, n2, n2)), dma((n2, n2, n2, n2, 6)), dma((n2,)), dma((n2, n3)), pltpu.SemaphoreType.REGULAR,
             *(vmem((n2, 6, *lead, width), F32)
               for lead_in, lead_out in (((*ring, dr), (n2, fr)), ((na, dr), (fr // n2,)))
-              for lead, width in ((lead_in, fs - pf), (lead_in, pf), (lead_out, dm - pf), (lead_out, pf))),
+              for lead, width in ((lead_in, fs - pf), (lead_in, pf), (lead_out, dm // n2), (lead_out, dm // n2))),
         ]
         hbm = pl.BlockSpec(memory_space=pl.ANY)
         whole = pl.BlockSpec(memory_space=pltpu.VMEM)

time: 110 us -> 110 us (level)
  no operation moved by 1% of the time
where the time goes in v14:
time: 110 us
  Pallas kernels  109 us (99%)
    pallas_call x1, Pallas kernels, body(): pl.pallas_call(kernel, out_shape=(vmem((rows, dm), BF), vmem((n2, dr, fd)...  108 us

profile of v14, /device:TPU:0, one launch (start us, length us, event | category | flops | bytes accessed | tf_op | source)
XLA Modules:
  0.0 109.8 jit_solution(1323814789143723331)
XLA Ops:
  0.6 108.1 %train_step.1 = (bf16[256,512]{1,0:T(8,128)(2,1)S(1)}, f32[2,8,2048]{2,1,0:T(8,128)S(1)}, f32[2,8,2048]{2,1,0:T(8,128)S(1)}, f32[2,32,512]{2,1,0:T(8,128)S(1)}) custom-call(bf16[256,512]{1,0:T(8,128)(2,1)} %bitcast.17, bf16[256,512]{1,0:T(8,128)(2,1)} %bitcast.18, bf16[2,8,2048]{2,1,0:T(8,128)(2,1)} %bitcast.19, bf16[2,8,2048]{2,1,0:T(8,128)(2,1)} %bitcast.20, ...), custom_call_target="tpu_custom_call" | custom-call | tf_op jit(solution)/shard_map/train_step/pallas_call | solution.py:694
  108.7 0.9 hand_on.1

commit v15 on v14

--- a/solution.py
+++ b/solution.py
@@ -42,15 +42,16 @@
 
 def kernel(act, cot, wg_in, wi_in, wo_in, gact, gg, gi, go,
            wg, wi, wo, hb, eb, xo, ga, ng, f1, f2, f1s, f2s, us, ub, da, db, das, dbs, qs, gs, is_, os_,
-           gin0, gin1, gout0, gout1, fin, r3,
-           lsem, ag_s, ag_r, lg_r, mc_s, mc_r, rl_s, ga_s, ga_r, rs_s, rs_r, r3_s, r3_r, turn, *rg):
+           gout0, gout1, fin, r3,
+           lsem, ag_s, ag_r, lg_r, mc_s, mc_r, rl_s, ga_s, ga_r, rs_s, rs_r, r3_s, r3_r, turn, *more):
     dm, fd = wo.shape[-1], wg.shape[-1]
     dr, fr = dm // NL, fd // NL
     fs = fd // NA
     pf = fs // NA
     rows = act.shape[0]
     wts = (wg, wi, wo)
-    gin, gout = (gin0, gin1), (gout0, gout1)
+    gins, rg = more[:4], more[4:]
+    gin, gout = (gins[:2], gins[2:]), (gout0, gout1)
 
     p = lax.axis_index("stage")
     d = lax.axis_index("data")
@@ -326,11 +327,10 @@
     def split(width, second):
         return pl.ds(0, width - second), pl.ds(width - second, second)
 
-    IN_COLS, OUT_COLS = split(fs, pf), split(dm, dm // 2)
-
-    def keep(refs, v, place, tile, cols, first):
+    IN_COLS, OUT_COLS = (split(fs, fs // 2), split(fs, pf)), split(dm, dm // 2)
+
+    def keep(refs, lead, place, tile, cols, first):
         b, rest = place[0], place[1:]
-        lead = () if v is None else (v,)
         for colour in COLOURS:
             part = tile[..., cols[colour].start:cols[colour].start + cols[colour].size]
             at = lead + ((b, slice(None)) if colour == 0 else (slice(None), b)) + rest
@@ -345,7 +345,7 @@
             cols = pl.ds(i * 2 * pf, 2 * pf)
             g = mm_tn(us[v, some, :, cols].reshape(count, 2 * pf), eb[v, some].reshape(count, dm)).reshape(2, NA, fr, dm)
             for b in HALVES:
-                keep(gout, v, (2 * i + b,), g[b], OUT_COLS, OWN in slots)
+                keep(gout, (v,), (2 * i + b,), g[b], OUT_COLS, OWN in slots)
 
     def grad_in(v, slots):
         some, count = rows_of(slots)
@@ -354,19 +354,21 @@
                 cols = pl.ds(i * (dm // NA), dm // NA)
                 g = mm_tn(ng[v, some, :, cols].reshape(count, dm // NA), dref[some].reshape(count, fs)).reshape(NA, NA, dr, fs)
                 for y in QUARTERS:
-                    keep([ref.at[v, which] for ref in gin], None, (i + p * (y - i), y + p * (i - y)), g[y], IN_COLS, OWN in slots)
+                    keep(gin[v], (which,), (i + p * (y - i), y + p * (i - y)), g[y], IN_COLS[v], OWN in slots)
 
     IN, OUT = 0, 1
 
     def view(which, st, v, colour, t, half):
         own = jb if colour == 0 else xc
         if which == IN:
-            ref = gin[colour].at[v, half]
+            ref = gin[v][colour].at[half]
             return ref.at[t] if st == 0 else ref.at[own, t]
         ref = gout[colour].at[v]
         return ref.at[t, pl.ds(2 * half, 2)] if st == 0 else ref.at[own, t, pl.ds(half * (fr // 2), fr // 2)]
 
-    RECV = (((rg[0], rg[1]), (rg[2], rg[3])), ((rg[4], rg[5]), (rg[6], rg[7])))
+    def landing(v, st, which, colour):
+        return rg[4 * v + 2 * st + colour] if which == IN else rg[8 + 2 * st + colour].at[v]
+
     MERGED, DIRECT = ((0, OPP, PLUS, 0), (1, OPP, MINUS, 1)), ((1, PLUS, PLUS, 2), (0, MINUS, MINUS, 3))
     RELAYED = ((0, PLUS, PLUS, 4), (1, MINUS, MINUS, 5))
 
@@ -377,29 +379,29 @@
         for colour in COLOURS:
             q, to = axis_of(colour, st)
             for half, c, delta, slot in copies:
-                send(view(which, st, v, colour, rot(q, c), half), RECV[st][which][colour].at[v, slot],
+                send(view(which, st, v, colour, rot(q, c), half), landing(v, st, which, colour).at[slot],
                      rs_s.at[st, v, colour, which], rs_r.at[st, v, colour, which, slot], to(delta), p)
 
     def scatter_relay(v, which, st):
         for colour in COLOURS:
             q, _ = axis_of(colour, st)
-            recv = RECV[st][which][colour]
+            recv = landing(v, st, which, colour)
             for half, c, _, slot in RELAYED:
-                wait_recv(recv.at[v, slot - 4], rs_r.at[st, v, colour, which, slot - 4])
+                wait_recv(recv.at[slot - 4], rs_r.at[st, v, colour, which, slot - 4])
                 ref = view(which, st, v, colour, rot(q, c), half)
-                ref[...] = ref[...] + recv[v, slot - 4]
+                ref[...] = ref[...] + recv[slot - 4]
         scatter_send(v, which, st, RELAYED)
 
     def scatter_sum(v, which, st):
         for colour in COLOURS:
             q, _ = axis_of(colour, st)
-            recv = RECV[st][which][colour]
+            recv = landing(v, st, which, colour)
             for half in HALVES:
                 direct, merged = 3 - half, 4 + half
                 for slot in (direct, merged):
-                    wait_recv(recv.at[v, slot], rs_r.at[st, v, colour, which, slot])
+                    wait_recv(recv.at[slot], rs_r.at[st, v, colour, which, slot])
                 ref = view(which, st, v, colour, q, half)
-                ref[...] = ref[...] + recv[v, direct] + recv[v, merged]
+                ref[...] = ref[...] + recv[direct] + recv[merged]
 
     def scatter_turn(v, which):
         scatter_sum(v, which, 0)
@@ -414,7 +416,7 @@
         scatter_sum(v, IN, 1)
         for which in HALVES:
             for colour in COLOURS:
-                fin[v, :, which, :, IN_COLS[colour]] = gin[colour][(v, which, jb, xc) if colour == 0 else (v, which, xc, jb)]
+                fin[v, :, which, :, IN_COLS[v][colour]] = gin[v][colour][(which, jb, xc) if colour == 0 else (which, xc, jb)]
         for delta in (OPP, PLUS, MINUS):
             send(fin.at[v, rot(ja, delta)], r3.at[v, delta - 1], r3_s.at[v], r3_r.at[v, delta - 1], peer_a(delta), p)
 
@@ -551,7 +553,6 @@
         step(block_backward, 0, e_last[0])
         pass_on(spread_near, e_last, eb, 1, 0)
         pass_on(spread_far, e_last, eb, 1, 0)
-        step(spread_relay, hb, 0, 0)
         step(grad_in, 1, EARLY)
 
     step(spread_finish, hb, 0, 1)
@@ -573,6 +574,7 @@
 
     @on(1)
     def _():
+        step(spread_relay, hb, 0, 0)
         step(grad_first, 0, EARLY)
         step(spread_relay, eb, 1, 0)
         step(spread_finish, hb, 0, 0)
@@ -629,7 +631,7 @@
         for colour in COLOURS:
             for which in HALVES:
                 for st in HALVES:
-                    wait_send(RECV[st][which][colour].at[v], rs_s.at[st, v, colour, which])
+                    wait_send(landing(v, st, which, colour), rs_s.at[st, v, colour, which])
         wait_send(r3.at[v], r3_s.at[v])
         wait_send(hb.at[v, 0], rl_s.at[0, v])
         wait_send(hb.at[v, 0], rl_s.at[1, v])
@@ -669,6 +671,7 @@
         dma = pltpu.SemaphoreType.DMA
         n2, n3, na = NB, len(RING), NA
         ring = (na, na)
+        in_widths = (fs // n2, fs // n2, fs - pf, pf)
         scratch = [
             vmem((n2, na, *ring, dr, fd), BF), vmem((n2, na, *ring, dr, fd), BF), vmem((n2, na, *ring, fr, dm), BF),
             vmem((n2, na, rows, dm), BF), vmem((n2, na, rows, dm), BF), vmem((na, rows, dm), BF), vmem((rows, dm), BF),
@@ -680,14 +683,14 @@
             vmem((na, rows, fs), BF), vmem((na, rows, fs), BF),
             vmem((rows, dm), F32),
             vmem((n2, dm, fs), BF), vmem((n2, dm, fs), BF), vmem((fs, dm), BF),
-            *(vmem((n2, n2, *ring, na, dr, width), F32) for width in (fs - pf, pf)),
             *(vmem((n2, *ring, fr, width), F32) for width in (dm // n2, dm // n2)),
             vmem((n2, na, n2, dr, fs), F32), vmem((n2, n3, n2, dr, fs), F32),
             dma((n2, na)), dma((n2, n3, n3)), dma((n2, n3, n2, 6)), dma((n2, n3, n3 * na)), dma((5,)), dma((n2, n2, 7)), dma((n2, n2)), dma, dma,
             dma((n2, n2, n2, n2)), dma((n2, n2, n2, n2, 6)), dma((n2,)), dma((n2, n3)), pltpu.SemaphoreType.REGULAR,
-            *(vmem((n2, 6, *lead, width), F32)
-              for lead_in, lead_out in (((*ring, dr), (n2, fr)), ((na, dr), (fr // n2,)))
-              for lead, width in ((lead_in, fs - pf), (lead_in, pf), (lead_out, dm // n2), (lead_out, dm // n2))),
+            *(vmem((n2, *ring, na, dr, width), F32) for width in in_widths),
+            *(vmem((6, *lead, width), F32)
+              for pair in (in_widths[:2], in_widths[2:]) for lead in ((*ring, dr), (na, dr)) for width in pair),
+            *(vmem((n2, 6, *lead, dm // n2), F32) for lead in ((n2, fr), (fr // n2,)) for _ in range(n2)),
         ]
         hbm = pl.BlockSpec(memory_space=pl.ANY)
         whole = pl.BlockSpec(memory_space=pltpu.VMEM)

time: 110 us -> 114 us (1.036)
  Pallas kernels: 109 us -> 113 us
    pallas_call x1, Pallas kernels: 108 us -> 112 us  [body(): pl.pallas_call(kernel, out_shape=(vmem((rows, dm), BF), vmem((n2, dr, fd)...]
where the time goes in v15:
time: 114 us
  Pallas kernels  113 us (99%)
    pallas_call x1, Pallas kernels, body(): pl.pallas_call(kernel, out_shape=(vmem((rows, dm), BF), vmem((n2, dr, fd)...  112 us

profile of v15, /device:TPU:0, one launch (start us, length us, event | category | flops | bytes accessed | tf_op | source)
XLA Modules:
  0.0 113.8 jit_solution(3879081427499084000)
XLA Ops:
  0.6 112.1 %train_step.1 = (bf16[256,512]{1,0:T(8,128)(2,1)S(1)}, f32[2,8,2048]{2,1,0:T(8,128)S(1)}, f32[2,8,2048]{2,1,0:T(8,128)S(1)}, f32[2,32,512]{2,1,0:T(8,128)S(1)}) custom-call(bf16[256,512]{1,0:T(8,128)(2,1)} %bitcast.17, bf16[256,512]{1,0:T(8,128)(2,1)} %bitcast.18, bf16[2,8,2048]{2,1,0:T(8,128)(2,1)} %bitcast.19, bf16[2,8,2048]{2,1,0:T(8,128)(2,1)} %bitcast.20, ...), custom_call_target="tpu_custom_call" | custom-call | tf_op jit(solution)/shard_map/train_step/pallas_call | solution.py:697
  112.8 0.9 hand_on.1

commit v16 on v14

--- a/solution.py
+++ b/solution.py
@@ -326,7 +326,7 @@
     def split(width, second):
         return pl.ds(0, width - second), pl.ds(width - second, second)
 
-    IN_COLS, OUT_COLS = split(fs, pf), split(dm, dm // 2)
+    IN_COLS, OUT_COLS = split(fs, pf), split(dm, pf)
 
     def keep(refs, v, place, tile, cols, first):
         b, rest = place[0], place[1:]
@@ -506,6 +506,11 @@
         step(give_turn)
         step(spread_relay, hb, 0, 0)
 
+    @on(1)
+    def _():
+        pass_on(spread_far, h_mid, hb, 0, p)
+        step(spread_same, eb, 1, 1, mc_s.at[0])
+
     step(spread_own, hb, 0, 1)
     step(large_finish, 1, UP_MATS)
     step(block_gates, 1)
@@ -519,23 +524,24 @@
         step(spread_finish, hb, 0, 0)
         step(grad_first, 0, EARLY)
         step(grad_first, 0, LATE)
+        step(spread_relay, hb, 0, 1)
+        step(grad_first, 1, EARLY)
         step(spread_own, eb, 1, 1)
         pass_on(spread_far, h_mid, hb, 0, p)
         step(block_backward, 1, e_first[0])
         pass_on(spread_near, e_first, eb, 1, 0)
         pass_on(spread_far, e_first, eb, 1, 0)
-        step(spread_relay, hb, 0, 1)
+        step(spread_finish, hb, 0, 1)
+        step(grad_first, 1, LATE)
 
     @on(1)
     def _():
-        pass_on(spread_far, h_mid, hb, 0, p)
-        step(spread_same, eb, 1, 1, mc_s.at[0])
         step(block_backward, 1, e_first[0])
         pass_on(spread_near, e_first, eb, 1, 1)
         pass_on(spread_far, e_first, eb, 1, 1)
         step(spread_relay, hb, 0, 1)
-
-    step(grad_first, 1, EARLY)
+        step(grad_first, 1, EARLY)
+
     step(spread_relay, eb, 1, 1)
 
     step(grad_hidden, 1, EARLY)
@@ -551,11 +557,9 @@
         step(block_backward, 0, e_last[0])
         pass_on(spread_near, e_last, eb, 1, 0)
         pass_on(spread_far, e_last, eb, 1, 0)
-        step(spread_relay, hb, 0, 0)
         step(grad_in, 1, EARLY)
-
-    step(spread_finish, hb, 0, 1)
-    step(grad_first, 1, LATE)
+        step(spread_finish, hb, 0, 1)
+        step(grad_first, 1, LATE)
 
     step(spread_finish, eb, 1, 1)
     step(grad_hidden, 1, LATE)
@@ -573,6 +577,7 @@
 
     @on(1)
     def _():
+        step(spread_relay, hb, 0, 0)
         step(grad_first, 0, EARLY)
         step(spread_relay, eb, 1, 0)
         step(spread_finish, hb, 0, 0)
@@ -681,13 +686,13 @@
             vmem((rows, dm), F32),
             vmem((n2, dm, fs), BF), vmem((n2, dm, fs), BF), vmem((fs, dm), BF),
             *(vmem((n2, n2, *ring, na, dr, width), F32) for width in (fs - pf, pf)),
-            *(vmem((n2, *ring, fr, width), F32) for width in (dm // n2, dm // n2)),
+            *(vmem((n2, *ring, fr, width), F32) for width in (dm - pf, pf)),
             vmem((n2, na, n2, dr, fs), F32), vmem((n2, n3, n2, dr, fs), F32),
             dma((n2, na)), dma((n2, n3, n3)), dma((n2, n3, n2, 6)), dma((n2, n3, n3 * na)), dma((5,)), dma((n2, n2, 7)), dma((n2, n2)), dma, dma,
             dma((n2, n2, n2, n2)), dma((n2, n2, n2, n2, 6)), dma((n2,)), dma((n2, n3)), pltpu.SemaphoreType.REGULAR,
             *(vmem((n2, 6, *lead, width), F32)
               for lead_in, lead_out in (((*ring, dr), (n2, fr)), ((na, dr), (fr // n2,)))
-              for lead, width in ((lead_in, fs - pf), (lead_in, pf), (lead_out, dm // n2), (lead_out, dm // n2))),
+              for lead, width in ((lead_in, fs - pf), (lead_in, pf), (lead_out, dm - pf), (lead_out, pf))),
         ]
         hbm = pl.BlockSpec(memory_space=pl.ANY)
         whole = pl.BlockSpec(memory_space=pltpu.VMEM)

time: 110 us -> 111 us (level)
  no operation moved by 1% of the time
where the time goes in v16:
time: 111 us; the launch traced here: 110 us
  Pallas kernels  110 us (99%)
    pallas_call x1, Pallas kernels, body(): pl.pallas_call(kernel, out_shape=(vmem((rows, dm), BF), vmem((n2, dr, fd)...  109 us

profile of v16, /device:TPU:0, one launch (start us, length us, event | category | flops | bytes accessed | tf_op | source)
XLA Modules:
  0.0 110.4 jit_solution(17920893719784332925)
XLA Ops:
  0.6 108.7 %train_step.1 = (bf16[256,512]{1,0:T(8,128)(2,1)S(1)}, f32[2,8,2048]{2,1,0:T(8,128)S(1)}, f32[2,8,2048]{2,1,0:T(8,128)S(1)}, f32[2,32,512]{2,1,0:T(8,128)S(1)}) custom-call(bf16[256,512]{1,0:T(8,128)(2,1)} %bitcast.17, bf16[256,512]{1,0:T(8,128)(2,1)} %bitcast.18, bf16[2,8,2048]{2,1,0:T(8,128)(2,1)} %bitcast.19, bf16[2,8,2048]{2,1,0:T(8,128)(2,1)} %bitcast.20, ...), custom_call_target="tpu_custom_call" | custom-call | tf_op jit(solution)/shard_map/train_step/pallas_call | solution.py:699
  109.3 0.9 hand_on.1

commit v17 on v16

--- a/solution.py
+++ b/solution.py
@@ -521,13 +521,13 @@
         step(block_out, 1, h_late[0])
         pass_on(spread_near, h_late, hb, 0, 1)
         pass_on(spread_far, h_late, hb, 0, 1)
+        pass_on(spread_far, h_mid, hb, 0, p)
         step(spread_finish, hb, 0, 0)
         step(grad_first, 0, EARLY)
         step(grad_first, 0, LATE)
         step(spread_relay, hb, 0, 1)
         step(grad_first, 1, EARLY)
         step(spread_own, eb, 1, 1)
-        pass_on(spread_far, h_mid, hb, 0, p)
         step(block_backward, 1, e_first[0])
         pass_on(spread_near, e_first, eb, 1, 0)
         pass_on(spread_far, e_first, eb, 1, 0)
@@ -541,15 +541,13 @@
         pass_on(spread_far, e_first, eb, 1, 1)
         step(spread_relay, hb, 0, 1)
         step(grad_first, 1, EARLY)
+        step(spread_relay, hb, 0, 0)
 
     step(spread_relay, eb, 1, 1)
 
     step(grad_hidden, 1, EARLY)
     step(grad_out, 1, EARLY)
-
-    @on(0)
-    def _():
-        step(grad_in, 1, EARLY)
+    step(grad_in, 1, EARLY)
 
     @on(1)
     def _():
@@ -557,7 +555,6 @@
         step(block_backward, 0, e_last[0])
         pass_on(spread_near, e_last, eb, 1, 0)
         pass_on(spread_far, e_last, eb, 1, 0)
-        step(grad_in, 1, EARLY)
         step(spread_finish, hb, 0, 1)
         step(grad_first, 1, LATE)
 
@@ -577,7 +574,6 @@
 
     @on(1)
     def _():
-        step(spread_relay, hb, 0, 0)
         step(grad_first, 0, EARLY)
         step(spread_relay, eb, 1, 0)
         step(spread_finish, hb, 0, 0)

time: 111 us -> 111 us (level)
  no operation moved by 1% of the time
where the time goes in v17:
time: 111 us
  Pallas kernels  110 us (99%)
    pallas_call x1, Pallas kernels, body(): pl.pallas_call(kernel, out_shape=(vmem((rows, dm), BF), vmem((n2, dr, fd)...  110 us

profile of v17, /device:TPU:0, one launch (start us, length us, event | category | flops | bytes accessed | tf_op | source)
XLA Modules:
  0.0 111.2 jit_solution(8784021429591040719)
XLA Ops:
  0.6 109.5 %train_step.1 = (bf16[256,512]{1,0:T(8,128)(2,1)S(1)}, f32[2,8,2048]{2,1,0:T(8,128)S(1)}, f32[2,8,2048]{2,1,0:T(8,128)S(1)}, f32[2,32,512]{2,1,0:T(8,128)S(1)}) custom-call(bf16[256,512]{1,0:T(8,128)(2,1)} %bitcast.17, bf16[256,512]{1,0:T(8,128)(2,1)} %bitcast.18, bf16[2,8,2048]{2,1,0:T(8,128)(2,1)} %bitcast.19, bf16[2,8,2048]{2,1,0:T(8,128)(2,1)} %bitcast.20, ...), custom_call_target="tpu_custom_call" | custom-call | tf_op jit(solution)/shard_map/train_step/pallas_call | solution.py:695
  110.2 0.9 hand_on.1

commit v18 on v17

--- a/solution.py
+++ b/solution.py
@@ -541,7 +541,6 @@
         pass_on(spread_far, e_first, eb, 1, 1)
         step(spread_relay, hb, 0, 1)
         step(grad_first, 1, EARLY)
-        step(spread_relay, hb, 0, 0)
 
     step(spread_relay, eb, 1, 1)
 
@@ -555,6 +554,7 @@
         step(block_backward, 0, e_last[0])
         pass_on(spread_near, e_last, eb, 1, 0)
         pass_on(spread_far, e_last, eb, 1, 0)
+        step(spread_relay, hb, 0, 0)
         step(spread_finish, hb, 0, 1)
         step(grad_first, 1, LATE)
 

time: 111 us -> 110 us (level)
    pallas_call x1, Pallas kernels: 110 us -> 108 us  [body(): pl.pallas_call(kernel, out_shape=(vmem((rows, dm), BF), vmem((n2, dr, fd)...]
where the time goes in v18:
time: 110 us
  Pallas kernels  109 us (99%)
    pallas_call x1, Pallas kernels, body(): pl.pallas_call(kernel, out_shape=(vmem((rows, dm), BF), vmem((n2, dr, fd)...  108 us

profile of v18, /device:TPU:0, one launch (start us, length us, event | category | flops | bytes accessed | tf_op | source)
XLA Modules:
  0.0 109.6 jit_solution(15704922712011141604)
XLA Ops:
  0.6 107.9 %train_step.1 = (bf16[256,512]{1,0:T(8,128)(2,1)S(1)}, f32[2,8,2048]{2,1,0:T(8,128)S(1)}, f32[2,8,2048]{2,1,0:T(8,128)S(1)}, f32[2,32,512]{2,1,0:T(8,128)S(1)}) custom-call(bf16[256,512]{1,0:T(8,128)(2,1)} %bitcast.17, bf16[256,512]{1,0:T(8,128)(2,1)} %bitcast.18, bf16[2,8,2048]{2,1,0:T(8,128)(2,1)} %bitcast.19, bf16[2,8,2048]{2,1,0:T(8,128)(2,1)} %bitcast.20, ...), custom_call_target="tpu_custom_call" | custom-call | tf_op jit(solution)/shard_map/train_step/pallas_call | solution.py:695
  108.6 0.9 hand_on.1

commit v19 on v18

--- a/solution.py
+++ b/solution.py
@@ -452,11 +452,6 @@
     AFTER = (MINUS, OPP), (0, PLUS)
     step(direct_send, 0)
     step(small_send, 1, 0)
-
-    @on(0)
-    def _():
-        step(spread_same, hb, 0, 0, mc_s.at[0])
-
     step(direct_wait, 0)
     step(small_send, 0, 1)
     step(small_relay, 1, 0)
@@ -504,7 +499,6 @@
     @on(0)
     def _():
         step(give_turn)
-        step(spread_relay, hb, 0, 0)
 
     @on(1)
     def _():
@@ -522,17 +516,13 @@
         pass_on(spread_near, h_late, hb, 0, 1)
         pass_on(spread_far, h_late, hb, 0, 1)
         pass_on(spread_far, h_mid, hb, 0, p)
-        step(spread_finish, hb, 0, 0)
-        step(grad_first, 0, EARLY)
-        step(grad_first, 0, LATE)
-        step(spread_relay, hb, 0, 1)
-        step(grad_first, 1, EARLY)
+        step(spread_same, hb, 0, 0, mc_s.at[0])
         step(spread_own, eb, 1, 1)
         step(block_backward, 1, e_first[0])
         pass_on(spread_near, e_first, eb, 1, 0)
         pass_on(spread_far, e_first, eb, 1, 0)
-        step(spread_finish, hb, 0, 1)
-        step(grad_first, 1, LATE)
+        step(spread_relay, hb, 0, 1)
+        step(grad_first, 1, EARLY)
 
     @on(1)
     def _():
@@ -547,6 +537,12 @@
     step(grad_hidden, 1, EARLY)
     step(grad_out, 1, EARLY)
     step(grad_in, 1, EARLY)
+
+    @on(0)
+    def _():
+        step(spread_relay, hb, 0, 0)
+        step(spread_finish, hb, 0, 1)
+        step(grad_first, 1, LATE)
 
     @on(1)
     def _():
@@ -569,7 +565,10 @@
 
     @on(0)
     def _():
+        step(grad_first, 0, EARLY)
         step(spread_relay, eb, 1, 0)
+        step(spread_finish, hb, 0, 0)
+        step(grad_first, 0, LATE)
         step(spread_own, eb, 1, 0)
 
     @on(1)

time: 110 us -> 109 us (level)
  no operation moved by 1% of the time
where the time goes in v19:
time: 109 us
  Pallas kernels  108 us (99%)
    pallas_call x1, Pallas kernels, body(): pl.pallas_call(kernel, out_shape=(vmem((rows, dm), BF), vmem((n2, dr, fd)...  107 us

profile of v19, /device:TPU:0, one launch (start us, length us, event | category | flops | bytes accessed | tf_op | source)
XLA Modules:
  0.0 108.7 jit_solution(16667429092910105647)
XLA Ops:
  0.6 107.0 %train_step.1 = (bf16[256,512]{1,0:T(8,128)(2,1)S(1)}, f32[2,8,2048]{2,1,0:T(8,128)S(1)}, f32[2,8,2048]{2,1,0:T(8,128)S(1)}, f32[2,32,512]{2,1,0:T(8,128)S(1)}) custom-call(bf16[256,512]{1,0:T(8,128)(2,1)} %bitcast.17, bf16[256,512]{1,0:T(8,128)(2,1)} %bitcast.18, bf16[2,8,2048]{2,1,0:T(8,128)(2,1)} %bitcast.19, bf16[2,8,2048]{2,1,0:T(8,128)(2,1)} %bitcast.20, ...), custom_call_target="tpu_custom_call" | custom-call | tf_op jit(solution)/shard_map/train_step/pallas_call | solution.py:694
  107.6 0.9 hand_on.1

commit v20 on v19

--- a/solution.py
+++ b/solution.py
@@ -503,10 +503,14 @@
     @on(1)
     def _():
         pass_on(spread_far, h_mid, hb, 0, p)
-        step(spread_same, eb, 1, 1, mc_s.at[0])
 
     step(spread_own, hb, 0, 1)
     step(large_finish, 1, UP_MATS)
+
+    @on(1)
+    def _():
+        step(spread_same, eb, 1, 1, mc_s.at[0])
+
     step(block_gates, 1)
     step(large_finish, 1, OUT_MAT)
 

time: 109 us -> 109 us (level)
  no operation moved by 1% of the time
where the time goes in v20:
time: 109 us
  Pallas kernels  108 us (99%)
    pallas_call x1, Pallas kernels, body(): pl.pallas_call(kernel, out_shape=(vmem((rows, dm), BF), vmem((n2, dr, fd)...  107 us

profile of v20, /device:TPU:0, one launch (start us, length us, event | category | flops | bytes accessed | tf_op | source)
XLA Modules:
  0.0 109.0 jit_solution(18034485442520624322)
XLA Ops:
  0.6 107.3 %train_step.1 = (bf16[256,512]{1,0:T(8,128)(2,1)S(1)}, f32[2,8,2048]{2,1,0:T(8,128)S(1)}, f32[2,8,2048]{2,1,0:T(8,128)S(1)}, f32[2,32,512]{2,1,0:T(8,128)S(1)}) custom-call(bf16[256,512]{1,0:T(8,128)(2,1)} %bitcast.17, bf16[256,512]{1,0:T(8,128)(2,1)} %bitcast.18, bf16[2,8,2048]{2,1,0:T(8,128)(2,1)} %bitcast.19, bf16[2,8,2048]{2,1,0:T(8,128)(2,1)} %bitcast.20, ...), custom_call_target="tpu_custom_call" | custom-call | tf_op jit(solution)/shard_map/train_step/pallas_call | solution.py:698
  108.0 0.9 hand_on.1

commit v21 on v19

--- a/solution.py
+++ b/solution.py
@@ -580,14 +580,31 @@
 
     step(grad_hidden, 0, EARLY)
     step(grad_in, 0, EARLY)
+
+    @on(0)
+    def _():
+        step(scatter_relay, 1, OUT, 0)
+
     step(grad_out, 0, EARLY)
-    step(scatter_relay, 1, OUT, 0)
+
+    @on(0)
+    def _():
+        step(scatter_relay, 1, IN, 0)
+
+    @on(1)
+    def _():
+        step(scatter_relay, 1, OUT, 0)
+
     step(spread_finish, eb, 1, 0)
     step(grad_hidden, 0, LATE)
     step(grad_in, 0, LATE)
     step(scatter_send, 0, IN, 0, MERGED)
     step(grad_out, 0, LATE)
-    step(scatter_relay, 1, IN, 0)
+
+    @on(1)
+    def _():
+        step(scatter_relay, 1, IN, 0)
+
     step(scatter_send, 0, OUT, 0, MERGED)
     step(scatter_send, 0, IN, 0, DIRECT)
 

time: 109 us -> 109 us (level)
  no operation moved by 1% of the time
where the time goes in v21:
time: 109 us; the launch traced here: 108 us
  Pallas kernels  108 us (99%)
    pallas_call x1, Pallas kernels, body(): pl.pallas_call(kernel, out_shape=(vmem((rows, dm), BF), vmem((n2, dr, fd)...  107 us

profile of v21, /device:TPU:0, one launch (start us, length us, event | category | flops | bytes accessed | tf_op | source)
XLA Modules:
  0.0 108.4 jit_solution(11839614237950738016)
XLA Ops:
  0.6 106.7 %train_step.1 = (bf16[256,512]{1,0:T(8,128)(2,1)S(1)}, f32[2,8,2048]{2,1,0:T(8,128)S(1)}, f32[2,8,2048]{2,1,0:T(8,128)S(1)}, f32[2,32,512]{2,1,0:T(8,128)S(1)}) custom-call(bf16[256,512]{1,0:T(8,128)(2,1)} %bitcast.17, bf16[256,512]{1,0:T(8,128)(2,1)} %bitcast.18, bf16[2,8,2048]{2,1,0:T(8,128)(2,1)} %bitcast.19, bf16[2,8,2048]{2,1,0:T(8,128)(2,1)} %bitcast.20, ...), custom_call_target="tpu_custom_call" | custom-call | tf_op jit(solution)/shard_map/train_step/pallas_call | solution.py:711
  107.3 0.9 hand_on.1
